TPU v7x, 8 devices: a whole 2x2x1 slice. The times are simulated.
8 devices in a mesh: tp: 2 (over z, y), dp: 4 (over x, core).
Axes of the slice: x: 2, y: 2, z: 1, core: 2. Of those that a mesh axis runs over, the one named last changes fastest.
Arguments:
- x_in: bfloat16 [128, 4096], P('dp')
- w_gate: bfloat16 [4096, 11008], P('dp', 'tp')
- w_up: bfloat16 [4096, 11008], P('dp', 'tp')
- w_down: bfloat16 [11008, 4096], P('tp', 'dp')
- dy_in: bfloat16 [128, 4096], P('dp')
Outputs:
- output 1: bfloat16 [128, 4096], P('dp')
- output 2: bfloat16 [128, 4096], P('dp')
- output 3: float32 [4096, 11008], P('dp', 'tp')
- output 4: float32 [4096, 11008], P('dp', 'tp')
- output 5: float32 [11008, 4096], P('tp', 'dp')
All inputs are finite; a program needn't handle non-finite values.
Results may differ from a plain program's by a relative error of at most 0.001.
Values are sent between devices in bfloat16 or wider.
A program may use at most 1 GiB of HBM per device.

v0:
```python
import jax
import jax.numpy as jnp
from jax import lax
from jax.sharding import PartitionSpec as P


def solution(mesh):
    def device_pass(x_rows, gate_blk, up_blk, down_blk, dy_rows):
        x_cols = lax.all_to_all(x_rows, 'dp', 1, 0, tiled=True)
        gate_part = jnp.dot(x_cols, gate_blk, preferred_element_type=jnp.float32)
        up_part = jnp.dot(x_cols, up_blk, preferred_element_type=jnp.float32)
        gate_pre = lax.psum_scatter(gate_part, 'dp', scatter_dimension=0, tiled=True)
        up_pre = lax.psum_scatter(up_part, 'dp', scatter_dimension=0, tiled=True)
        sig_gate = jax.nn.sigmoid(gate_pre)
        silu_gate = gate_pre * sig_gate
        hidden = (silu_gate * up_pre).astype(jnp.bfloat16)
        hidden_all = lax.all_gather(hidden, 'dp', axis=0, tiled=True)
        out_part = jnp.dot(hidden_all, down_blk, preferred_element_type=jnp.float32)
        y_cols = (x_cols.astype(jnp.float32) + lax.psum(out_part, 'tp')).astype(jnp.bfloat16)
        y_rows = lax.all_to_all(y_cols, 'dp', 0, 1, tiled=True)
        dy_cols = lax.all_to_all(dy_rows, 'dp', 1, 0, tiled=True)
        grad_part = jnp.einsum('td,fd->tf', dy_cols, down_blk, preferred_element_type=jnp.float32)
        grad_h = lax.psum_scatter(grad_part, 'dp', scatter_dimension=0, tiled=True)
        d_gate = (grad_h * up_pre * sig_gate * (1.0 + gate_pre * (1.0 - sig_gate))).astype(jnp.bfloat16)
        d_up = (grad_h * silu_gate).astype(jnp.bfloat16)
        gate_all = lax.all_gather(d_gate, 'dp', axis=0, tiled=True)
        up_all = lax.all_gather(d_up, 'dp', axis=0, tiled=True)
        dx_part = (jnp.einsum('tf,df->td', gate_all, gate_blk, preferred_element_type=jnp.float32)
                   + jnp.einsum('tf,df->td', up_all, up_blk, preferred_element_type=jnp.float32))
        dx_cols = (dy_cols.astype(jnp.float32) + lax.psum(dx_part, 'tp')).astype(jnp.bfloat16)
        dx_rows = lax.all_to_all(dx_cols, 'dp', 0, 1, tiled=True)
        dw_gate = jnp.einsum('td,tf->df', x_cols, gate_all, preferred_element_type=jnp.float32)
        dw_up = jnp.einsum('td,tf->df', x_cols, up_all, preferred_element_type=jnp.float32)
        dw_down = jnp.einsum('tf,td->fd', hidden_all, dy_cols, preferred_element_type=jnp.float32)
        return y_rows, dx_rows, dw_gate, dw_up, dw_down

    row_spec = P('dp', None)
    weight_spec = P('dp', 'tp')
    down_spec = P('tp', 'dp')
    return jax.shard_map(device_pass, mesh=mesh,
                         in_specs=(row_spec, weight_spec, weight_spec, down_spec, row_spec),
                         out_specs=(row_spec, row_spec, weight_spec, weight_spec, down_spec),
                         check_vma=False)
```

profile of v0, /device:TPU:0, one launch (start us, length us, event | category | flops | bytes accessed | tf_op | source)
XLA Modules:
  0.0 300.1 jit_solution(6156998081750245850)
XLA Ops:
  7.2 0.0 copy-start.3
  7.2 0.0 reduce-scatter.8.cloned.1.call-start
  7.2 1.0 copy.22
  8.2 10.4 %all_to_all.76 = bf16[32,4,1024]{2,0,1:T(8,128)(2,1)S(1)} all-to-all(bf16[32,4,1024]{2,0,1:T(8,128)(2,1)S(1)} %bitcast.54), channel_id=1, replica_groups=mesh['tp'=2,'dp'=4] {'dp'}, dimensions={1} | all-to-all | bytes 524288 | tf_op jit(solution)/shard_map/all_to_all | solution.py:21
  18.6 9.5 %fusion.4 = f32[128,5504]{1,0:T(8,128)} fusion(bf16[128,1024]{1,0:T(8,128)(2,1)S(1)} %bitcast.50, bf16[5504,1024]{1,0:T(8,128)(2,1)} %param.8), kind=kOutput, calls=%fused_computation.15 | convolution fusion | flops 1442840576 | bytes 14352384 | tf_op jit(solution)/shard_map/td,fd->tf/dot_general | solution.py:22
  28.1 0.0 reduce-scatter.8.cloned.1.call-update
  28.2 0.0 reduce-scatter.6.cloned.1.call-start
  28.2 0.0 copy-done.3
  28.3 8.4 %all_to_all.77 = bf16[32,4,1024]{2,0,1:T(8,128)(2,1)S(1)} all-to-all(bf16[32,4,1024]{2,0,1:T(8,128)(2,1)S(1)} %bitcast.55), channel_id=1, replica_groups=mesh['tp'=2,'dp'=4] {'dp'}, dimensions={1} | all-to-all | bytes 524288 | tf_op jit(solution)/shard_map/all_to_all | solution.py:9
  36.6 7.4 %fusion.2 = f32[128,5504]{1,0:T(8,128)} fusion(bf16[128,1024]{1,0:T(8,128)(2,1)S(1)} %bitcast.46, bf16[1024,5504]{1,0:T(8,128)(2,1)} %param.7), kind=kOutput, calls=%fused_computation.13 | convolution fusion | flops 1442840576 | bytes 14352384 | tf_op jit(solution)/shard_map/dot_general | solution.py:11
  44.1 0.0 reduce-scatter.6.cloned.1.call-update
  44.1 0.0 reduce-scatter.4.cloned.1.call-start
  44.2 7.5 %fusion.1 = f32[128,5504]{1,0:T(8,128)} fusion(bf16[128,1024]{1,0:T(8,128)(2,1)S(1)} %bitcast.47, bf16[1024,5504]{1,0:T(8,128)(2,1)} %param.6), kind=kOutput, calls=%fused_computation.12 | convolution fusion | flops 1442840576 | bytes 14352384 | tf_op jit(solution)/shard_map/dot_general | solution.py:10
  51.6 0.0 reduce-scatter.4.cloned.1.call-update
  51.7 0.0 all-gather.4.cloned.1.call-start
  51.7 6.6 %reduce-scatter.8.cloned.1.call-done = f32[32,5504]{1,0:T(8,128)} async-done(((f32[128,5504]{1,0:T(8,128)}), f32[32,5504]{1,0:T(8,128)}) %reduce-scatter.8.cloned.1.call-update) | async-done | bytes 704528 | tf_op jit(solution)/shard_map/reduce_scatter | solution.py:23
  58.3 33.1 %reduce-scatter.6.cloned.1.call-done = f32[32,5504]{1,0:T(8,128)} async-done(((f32[128,5504]{1,0:T(8,128)}), f32[32,5504]{1,0:T(8,128)}) %reduce-scatter.6.cloned.1.call-update) | async-done | bytes 704528 | tf_op jit(solution)/shard_map/reduce_scatter | solution.py:13
  91.3 33.1 %reduce-scatter.4.cloned.1.call-done = f32[32,5504]{1,0:T(8,128)} async-done(((f32[128,5504]{1,0:T(8,128)}), f32[32,5504]{1,0:T(8,128)}) %reduce-scatter.4.cloned.1.call-update) | async-done | bytes 704528 | tf_op jit(solution)/shard_map/reduce_scatter | solution.py:12
  124.4 2.8 multiply_convert_fusion
  127.2 0.0 all-gather.4.cloned.1.call-update
  127.2 0.0 all-gather.6.cloned.1.call-start
  127.3 0.5 all-gather.6.cloned.1.call-update
  127.8 0.0 all-gather.8.cloned.1.call-start
  127.9 0.5 all-gather.8.cloned.1.call-update
  128.4 0.2 all-reduce.3.cloned.1.call-start
  128.6 14.5 %all-gather.4.cloned.1.call-done = bf16[128,5504]{1,0:T(8,128)(2,1)} async-done(((bf16[32,5504]{1,0:T(8,128)(2,1)}), bf16[128,5504]{1,0:T(8,128)(2,1)}) %all-gather.4.cloned.1.call-update) | async-done | bytes 1409040 | tf_op jit(solution)/shard_map/all_gather | solution.py:17
  143.1 7.1 %fusion.3 = f32[128,1024]{1,0:T(8,128)} fusion(bf16[128,5504]{1,0:T(8,128)(2,1)} %all-gather.4.cloned.1.call-done, bf16[5504,1024]{1,0:T(8,128)(2,1)} %param.8), kind=kOutput, calls=%fused_computation.14 | convolution fusion | flops 1442840576 | bytes 13205504 | tf_op jit(solution)/shard_map/dot_general | solution.py:18
  150.2 10.6 %all-gather.6.cloned.1.call-done = bf16[128,5504]{1,0:T(8,128)(2,1)} async-done(((bf16[32,5504]{1,0:T(8,128)(2,1)}), bf16[128,5504]{1,0:T(8,128)(2,1)}) %all-gather.6.cloned.1.call-update) | async-done | bytes 1409040 | tf_op jit(solution)/shard_map/all_gather | solution.py:26
  160.8 8.3 %fusion.5 = f32[128,1024]{1,0:T(8,128)S(1)} fusion(bf16[128,5504]{1,0:T(8,128)(2,1)} %all-gather.6.cloned.1.call-done, bf16[1024,5504]{1,0:T(8,128)(2,1)} %param.6), kind=kOutput, calls=%fused_computation.16 | convolution fusion | flops 1442840576 | bytes 13205504 | tf_op jit(solution)/shard_map/tf,df->td/dot_general | solution.py:28
  169.1 9.4 %all-gather.8.cloned.1.call-done = bf16[128,5504]{1,0:T(8,128)(2,1)} async-done(((bf16[32,5504]{1,0:T(8,128)(2,1)}), bf16[128,5504]{1,0:T(8,128)(2,1)}) %all-gather.8.cloned.1.call-update) | async-done | bytes 1409040 | tf_op jit(solution)/shard_map/all_gather | solution.py:27
  178.6 9.2 %convolution_add_fusion = f32[128,1024]{1,0:T(8,128)} fusion(f32[128,1024]{1,0:T(8,128)S(1)} %fusion.5, bf16[128,5504]{1,0:T(8,128)(2,1)} %all-gather.8.cloned.1.call-done, bf16[1024,5504]{1,0:T(8,128)(2,1)} %param.7), kind=kOutput, calls=%fused_computation.2 | convolution fusion | flops 1442971648 | bytes 13729792 | tf_op jit(solution)/shard_map/tf,df->td/dot_general | solution.py:29
  187.8 0.0 all-reduce.3.cloned.1.call-update
  187.8 0.0 copy-done.2
  187.8 0.0 copy-start.1
  187.8 9.7 %convolution_bitcast_fusion = f32[1024,5504]{0,1:T(8,128)} fusion(bf16[128,5504]{1,0:T(8,128)(2,1)S(1)} %copy-done.2, bf16[128,1024]{1,0:T(8,128)(2,1)S(1)} %bitcast.48), kind=kOutput, calls=%fused_computation | convolution fusion | flops 1442840576 | bytes 24215552 | tf_op jit(solution)/shard_map/td,tf->df/dot_general | solution.py:33
  197.5 9.2 %convolution_bitcast_fusion.1 = f32[1024,5504]{0,1:T(8,128)} fusion(bf16[128,5504]{1,0:T(8,128)(2,1)S(1)} %copy-done.1, bf16[128,1024]{1,0:T(8,128)(2,1)S(1)} %bitcast.49), kind=kOutput, calls=%fused_computation.1 | convolution fusion | flops 1442840576 | bytes 24215552 | tf_op jit(solution)/shard_map/td,tf->df/dot_general | solution.py:32
  206.7 15.5 %all-reduce.3.cloned.1.call-done = (f32[128,1024]{1,0:T(8,128)}, f32[128,1024]{1,0:T(8,128)}) async-done(((f32[128,1024]{1,0:T(8,128)}, f32[128,1024]{1,0:T(8,128)}), (f32[128,1024]{1,0:T(8,128)}, f32[128,1024]{1,0:T(8,128)})) %all-reduce.3.cloned.1.call-update) | async-done | bytes 1048592 | tf_op jit(solution)/shard_map/psum | solution.py:19
  222.2 1.8 add_convert_fusion.1
  224.0 3.4 %all-to-all-start.1 = ((bf16[4,32,1024]{2,1,0:T(8,128)(2,1)}), bf16[4,32,1024]{2,1,0:T(8,128)(2,1)S(1)}, u32[]{:S(2)}, u32[]{:S(2)}) async-start(bf16[4,32,1024]{2,1,0:T(8,128)(2,1)} %bitcast.3), calls=%async_computation.3 | async-start | bytes 524288 | tf_op jit(solution)/shard_map/all_to_all | solution.py:20
  227.4 1.8 add_convert_fusion
  229.2 4.0 %all-to-all-done.1 = bf16[4,32,1024]{2,1,0:T(8,128)(2,1)S(1)} async-done(((bf16[4,32,1024]{2,1,0:T(8,128)(2,1)}), bf16[4,32,1024]{2,1,0:T(8,128)(2,1)S(1)}, u32[]{:S(2)}, u32[]{:S(2)}) %all-to-all-start.1) | async-done | bytes 262176 | tf_op jit(solution)/shard_map/all_to_all | solution.py:20
  233.2 3.4 %all-to-all-start.3 = ((bf16[4,32,1024]{2,1,0:T(8,128)(2,1)}), bf16[4,32,1024]{2,1,0:T(8,128)(2,1)S(1)}, u32[]{:S(2)}, u32[]{:S(2)}) async-start(bf16[4,32,1024]{2,1,0:T(8,128)(2,1)} %bitcast.8), calls=%async_computation.6 | async-start | bytes 524288 | tf_op jit(solution)/shard_map/all_to_all | solution.py:31
  236.6 9.7 %fusion.6 = f32[5504,1024]{1,0:T(8,128)} fusion(bf16[128,5504]{1,0:T(8,128)(2,1)S(1)} %copy-done, bf16[128,1024]{1,0:T(8,128)(2,1)S(1)} %bitcast.51), kind=kOutput, calls=%fused_computation.17 | convolution fusion | flops 1442840576 | bytes 24215552 | tf_op jit(solution)/shard_map/tf,td->fd/dot_general | solution.py:34
  246.3 22.7 %copy.15 = f32[1024,5504]{1,0:T(8,128)} copy(f32[1024,5504]{0,1:T(8,128)} %convolution_bitcast_fusion) | data formatting | bytes 45088768
  269.1 22.7 %copy.14 = f32[1024,5504]{1,0:T(8,128)} copy(f32[1024,5504]{0,1:T(8,128)} %convolution_bitcast_fusion.1) | data formatting | bytes 45088768
  291.8 0.7 copy.18
  292.5 0.0 all-to-all-done.3
  292.5 0.7 copy.19
  (5 shorter events, 0.0 us)
Async XLA Ops:
  7.2 21.1 %copy-start.3 = (bf16[32,4096]{1,0:T(8,128)(2,1)S(1)}, bf16[32,4096]{1,0:T(8,128)(2,1)}, u32[]{:S(2)}) copy-start(bf16[32,4096]{1,0:T(8,128)(2,1)} %param.5) | copy-start | bytes 786436
  7.2 51.1 %reduce-scatter.8.cloned.1.call-start = ((), (), s32[]{:S(2)}) async-start(), calls=%async_computation.10 | async-start | bytes 3522560 | tf_op jit(solution)/shard_map/reduce_scatter | solution.py:23
  28.2 63.2 %reduce-scatter.6.cloned.1.call-start = ((), (), s32[]{:S(2)}) async-start(), calls=%async_computation.8 | async-start | bytes 3522560 | tf_op jit(solution)/shard_map/reduce_scatter | solution.py:13
  44.1 80.3 %reduce-scatter.4.cloned.1.call-start = ((), (), s32[]{:S(2)}) async-start(), calls=%async_computation.7 | async-start | bytes 3522560 | tf_op jit(solution)/shard_map/reduce_scatter | solution.py:12
  51.7 91.5 %all-gather.4.cloned.1.call-start = ((), (), s32[]{:S(2)}) async-start(), calls=%async_computation.9 | async-start | bytes 1761280 | tf_op jit(solution)/shard_map/all_gather | solution.py:17
  127.2 33.6 %all-gather.6.cloned.1.call-start = ((), (), s32[]{:S(2)}) async-start(), calls=%async_computation.11 | async-start | bytes 1761280 | tf_op jit(solution)/shard_map/all_gather | solution.py:26
  127.8 50.8 %all-gather.8.cloned.1.call-start = ((), (), s32[]{:S(2)}) async-start(), calls=%async_computation.12 | async-start | bytes 1761280 | tf_op jit(solution)/shard_map/all_gather | solution.py:27
  128.4 93.8 %all-reduce.3.cloned.1.call-start = ((), (), s32[]{:S(2)}) async-start(), calls=%async_computation.13 | async-start | bytes 2097152 | tf_op jit(solution)/shard_map/psum | solution.py:19
  178.6 9.2 %copy-start.2 = (bf16[128,5504]{1,0:T(8,128)(2,1)S(1)}, bf16[128,5504]{1,0:T(8,128)(2,1)}, u32[]{:S(2)}) copy-start(bf16[128,5504]{1,0:T(8,128)(2,1)} %all-gather.8.cloned.1.call-done) | copy-start | bytes 4227076
  187.8 9.7 %copy-start.1 = (bf16[128,5504]{1,0:T(8,128)(2,1)S(1)}, bf16[128,5504]{1,0:T(8,128)(2,1)}, u32[]{:S(2)}) copy-start(bf16[128,5504]{1,0:T(8,128)(2,1)} %all-gather.6.cloned.1.call-done) | copy-start | bytes 4227076
  197.5 39.1 %copy-start = (bf16[128,5504]{1,0:T(8,128)(2,1)S(1)}, bf16[128,5504]{1,0:T(8,128)(2,1)}, u32[]{:S(2)}) copy-start(bf16[128,5504]{1,0:T(8,128)(2,1)} %all-gather.4.cloned.1.call-done) | copy-start | bytes 4227076
  224.0 9.2 %all-to-all-start.1 = ((bf16[4,32,1024]{2,1,0:T(8,128)(2,1)}), bf16[4,32,1024]{2,1,0:T(8,128)(2,1)S(1)}, u32[]{:S(2)}, u32[]{:S(2)}) async-start(bf16[4,32,1024]{2,1,0:T(8,128)(2,1)} %bitcast.3), calls=%async_computation.3 | async-start | bytes 524288 | tf_op jit(solution)/shard_map/all_to_all | solution.py:20
  233.2 59.3 %all-to-all-start.3 = ((bf16[4,32,1024]{2,1,0:T(8,128)(2,1)}), bf16[4,32,1024]{2,1,0:T(8,128)(2,1)S(1)}, u32[]{:S(2)}, u32[]{:S(2)}) async-start(bf16[4,32,1024]{2,1,0:T(8,128)(2,1)} %bitcast.8), calls=%async_computation.6 | async-start | bytes 524288 | tf_op jit(solution)/shard_map/all_to_all | solution.py:31
Sparse Core Ops, SparseCore 0:
  28.3 29.9 reduce-scatter.7
  61.4 29.9 reduce-scatter.5
  94.5 29.9 reduce-scatter.3
  127.3 15.7 all-gather.3
  145.1 15.7 all-gather.5
  162.8 15.7 all-gather.7
  187.9 34.2 all-reduce.2
where the time goes:
time: 301 us; the launch traced here: 300 us
  waiting for transfers between devices  128 us (43%)
  matrix products  77.6 us (26%)
  local copies, waits for them, and re-layouts  47.9 us (16%)
  blocking collectives  18.8 us (6%)
  between operations  14.2 us (5%)
  starting transfers between devices  7.27 us (2%)
  other arithmetic  6.39 us (2%)
    unnamed x10, local copies, waits for them, and re-layouts  45.5 us
    reduce_scatter x1, waiting for transfers between devices, device_pass(): lax.psum_scatter(gate_part, 'dp', scatter_dimension=0, tiled=True)  33.1 us
    reduce_scatter x1, waiting for transfers between devices, device_pass(): up_pre = lax.psum_scatter(up_part, 'dp', scatter_dimension=0, tiled=True)  33.1 us
    psum x1, waiting for transfers between devices, device_pass(): lax.psum(out_part, 'tp')  15.5 us
    all_gather x1, waiting for transfers between devices, device_pass(): hidden_all = lax.all_gather(hidden, 'dp', axis=0, tiled=True)  14.5 us
    all_gather x1, waiting for transfers between devices, device_pass(): gate_all = lax.all_gather(d_gate, 'dp', axis=0, tiled=True)  10.6 us
    all_to_all x1, blocking collectives, device_pass(): dy_cols = lax.all_to_all(dy_rows, 'dp', 1, 0, tiled=True)  10.4 us
    dot_general x1, matrix products, device_pass(): jnp.einsum('td,tf->df', x_cols, up_all, preferred_element_type=jnp.float32)  9.73 us
  transfers between devices with their start and end apart: 9, of which 8 were waited for; matrix products, arithmetic and copies ran while one was open for 36% of the time, Pallas kernels for 0%

commit v1 on v0

v1 whole, which is shorter than its diff:
```python
import functools

import jax
import jax.numpy as jnp
from jax import lax
from jax.experimental import pallas as pl
from jax.experimental.pallas import tpu as pltpu
from jax.sharding import PartitionSpec as P

MESH = pl.DeviceIdType.MESH
F32, BF16 = jnp.float32, jnp.bfloat16
VMEM_CAP = 67043328
WIDTHS = (256, 768, 1024, 1024, 1024, 1024, 384)
STARTS = tuple(sum(WIDTHS[:k]) for k in range(len(WIDTHS)))
NCH = len(WIDTHS)
HID = sum(WIDTHS)


def column_tiles(start, width, body):
    full = width // 256

    def step(i, carry):
        body(pl.multiple_of(start + i * 256, 128), 256)
        return carry

    lax.fori_loop(0, full, step, 0)
    if width % 256:
        body(start + full * 256, width % 256)


def exchange_kernel(x_ref, dy_ref, wg_hbm, wu_hbm, wd_hbm,
                    act_out, cols_out, keep_out, give_out, kept_cols_out,
                    wg, wu, wd, part, from_sib, from_opp, act, cols, acc,
                    w_sem, x_send, x_recv, s1_send, s1_recv, s2_send, s2_recv,
                    sib_send, sib_recv, opp_send, opp_recv, fwd_send, fwd_recv, out_sem, col_sem, acc_sem):
    t = lax.axis_index('tp')
    d = lax.axis_index('dp')
    cx, c = d // 2, lax.rem(d, 2)
    sib = 2 * cx + (1 - c)
    opp = 2 * (1 - cx) + c
    far = 2 * (1 - cx) + (1 - c)
    own_row = pl.multiple_of(32 * (2 * c + cx), 32)
    opp_row = pl.multiple_of(32 * (2 * c + 1 - cx), 32)
    sib_row = pl.multiple_of(32 * (2 * (1 - c) + cx), 32)
    far_row = pl.multiple_of(32 * (2 * (1 - c) + 1 - cx), 32)
    sib_half = pl.multiple_of(64 * (1 - c), 64)

    def weight_copies(k):
        cs = pl.ds(STARTS[k], WIDTHS[k])
        return (pltpu.make_async_copy(wg_hbm.at[:, cs], wg.at[:, cs], w_sem.at[0, k]),
                pltpu.make_async_copy(wu_hbm.at[:, cs], wu.at[:, cs], w_sem.at[1, k]),
                pltpu.make_async_copy(wd_hbm.at[cs, :], wd.at[cs, :], w_sem.at[2, k]))

    for k in range(NCH):
        for copy in weight_copies(k):
            copy.start()

    barrier = pltpu.get_barrier_semaphore()
    peers = (sib, opp, far)
    for p in peers:
        pl.semaphore_signal(barrier, inc=1, device_id={'dp': p}, device_id_type=MESH)
    pl.semaphore_wait(barrier, 3)

    def token_copy(i, ref, q, row):
        block = pl.ds(pl.multiple_of(1024 * peers[q], 128), 1024)
        return pltpu.make_async_remote_copy(
            src_ref=ref.at[:, block], dst_ref=cols.at[i, pl.ds(row, 32), :],
            send_sem=x_send.at[i, q], recv_sem=x_recv.at[i, q],
            device_id={'dp': peers[q]}, device_id_type=MESH)

    own_block = pl.ds(pl.multiple_of(1024 * d, 128), 1024)
    for i, ref in enumerate((x_ref, dy_ref)):
        for q in (2, 1, 0):
            token_copy(i, ref, q, own_row).start()
    for i, ref in enumerate((x_ref, dy_ref)):
        cols[i, pl.ds(own_row, 32), :] = ref[:, own_block]
    arrival_rows = (sib_row, opp_row, far_row)

    def token_wait(i, ref):
        for q in range(3):
            token_copy(i, ref, q, arrival_rows[q]).wait_recv()

    def s1(k):
        cs = pl.ds(STARTS[k], WIDTHS[k])
        return pltpu.make_async_remote_copy(
            src_ref=part.at[:, pl.ds(sib_half, 64), cs], dst_ref=from_sib.at[:, :, cs],
            send_sem=s1_send.at[k], recv_sem=s1_recv.at[k], device_id={'dp': sib}, device_id_type=MESH)

    def s2(k):
        cs = pl.ds(STARTS[k], WIDTHS[k])
        return pltpu.make_async_remote_copy(
            src_ref=part.at[:, pl.ds(opp_row, 32), cs], dst_ref=from_opp.at[:, :, cs],
            send_sem=s2_send.at[k], recv_sem=s2_recv.at[k], device_id={'dp': opp}, device_id_type=MESH)

    def act_copy(k, src_row, dst_row, send, recv, to):
        cs = pl.ds(STARTS[k], WIDTHS[k])
        return pltpu.make_async_remote_copy(
            src_ref=act.at[:, pl.ds(src_row, 32), cs], dst_ref=act.at[:, pl.ds(dst_row, 32), cs],
            send_sem=send.at[k], recv_sem=recv.at[k], device_id={'dp': to}, device_id_type=MESH)

    def partials(k):
        copies = weight_copies(k)
        copies[0].wait()
        copies[1].wait()
        if k == 0:
            token_wait(0, x_ref)

        def first(col, width):
            cs = pl.ds(col, width)
            part[0, :, cs] = jnp.dot(cols[0], wg[:, cs], preferred_element_type=F32)
            part[1, :, cs] = jnp.dot(cols[0], wu[:, cs], preferred_element_type=F32)

        def second(col, width):
            cs = pl.ds(col, width)
            part[2, :, cs] = lax.dot_general(cols[1], wd[cs, :], (((1,), (1,)), ((), ())),
                                             preferred_element_type=F32)

        def both(col, width):
            first(col, width)
            second(col, width)

        if k == 0:
            column_tiles(STARTS[k], WIDTHS[k], first)
            copies[2].wait()
            token_wait(1, dy_ref)
            column_tiles(STARTS[k], WIDTHS[k], second)
        else:
            copies[2].wait()
            column_tiles(STARTS[k], WIDTHS[k], both)
        s1(k).start()

    def chip_sum(k):
        s1(k).wait_recv()
        half = pl.multiple_of(32 * (1 - cx), 32)

        def add(col, width):
            cs = pl.ds(col, width)
            for i in range(3):
                part[i, pl.ds(opp_row, 32), cs] += from_sib[i, pl.ds(half, 32), cs]

        column_tiles(STARTS[k], WIDTHS[k], add)
        s2(k).start()

    def activations(k):
        s2(k).wait_recv()
        half = pl.multiple_of(32 * cx, 32)

        def body(col, width):
            cs = pl.ds(col, width)
            own = pl.ds(own_row, 32)
            mine = [part[i, own, cs] + from_sib[i, pl.ds(half, 32), cs] for i in range(3)]
            a, b, g = [mine[i] + from_opp[i, :, cs] for i in range(3)]
            s = jax.nn.sigmoid(a)
            silu = a * s
            act[0, own, cs] = (silu * b).astype(BF16)
            act[1, own, cs] = (g * b * s * (1.0 + a * (1.0 - s))).astype(BF16)
            act[2, own, cs] = (g * silu).astype(BF16)

        column_tiles(STARTS[k], WIDTHS[k], body)
        act_copy(k, own_row, own_row, opp_send, opp_recv, opp).start()
        act_copy(k, own_row, own_row, sib_send, sib_recv, sib).start()

    def forward(k):
        act_copy(k, own_row, opp_row, opp_send, opp_recv, opp).wait_recv()
        act_copy(k, opp_row, opp_row, fwd_send, fwd_recv, sib).start()

    def act_store(k):
        cs = pl.ds(STARTS[k], WIDTHS[k])
        return pltpu.make_async_copy(act.at[:, :, cs], act_out.at[:, :, cs], out_sem.at[k])

    def outputs(k):
        act_copy(k, own_row, sib_row, sib_send, sib_recv, sib).wait_recv()
        act_copy(k, opp_row, far_row, fwd_send, fwd_recv, sib).wait_recv()
        act_store(k).start()
        cs = pl.ds(STARTS[k], WIDTHS[k])

        def step(n, carry):
            ns = pl.ds(pl.multiple_of(n * 256, 256), 256)
            y = jnp.dot(act[0, :, cs], wd[cs, ns], preferred_element_type=F32)
            dx = (lax.dot_general(act[1, :, cs], wg[ns, cs], (((1,), (1,)), ((), ())), preferred_element_type=F32)
                  + lax.dot_general(act[2, :, cs], wu[ns, cs], (((1,), (1,)), ((), ())), preferred_element_type=F32))
            if k == 0:
                acc[0, :, ns] = y
                acc[1, :, ns] = dx
            else:
                acc[0, :, ns] += y
                acc[1, :, ns] += dx
            return carry

        lax.fori_loop(0, 4, step, 0)

    for k in range(NCH):
        partials(k)
        if k == 0:
            store_cols = pltpu.make_async_copy(cols, cols_out, col_sem.at[0])
            store_cols.start()
            store_kept = pltpu.make_async_copy(cols.at[:, pl.ds(pl.multiple_of(64 * t, 64), 64), :],
                                               kept_cols_out, col_sem.at[1])
            store_kept.start()
        if k >= 1:
            chip_sum(k - 1)
    chip_sum(NCH - 1)
    for k in range(NCH):
        activations(k)
    for k in range(NCH):
        forward(k)
        if k >= 1:
            outputs(k - 1)
    outputs(NCH - 1)
    store_keep = pltpu.make_async_copy(acc.at[:, pl.ds(pl.multiple_of(64 * t, 64), 64), :], keep_out, acc_sem.at[0])
    store_give = pltpu.make_async_copy(acc.at[:, pl.ds(pl.multiple_of(64 * (1 - t), 64), 64), :], give_out,
                                       acc_sem.at[1])
    store_give.start()
    store_keep.start()
    for i, ref in enumerate((x_ref, dy_ref)):
        for q in range(3):
            token_copy(i, ref, q, own_row).wait_send()
    for k in range(NCH):
        s1(k).wait_send()
        s2(k).wait_send()
        act_copy(k, own_row, own_row, opp_send, opp_recv, opp).wait_send()
        act_copy(k, own_row, own_row, sib_send, sib_recv, sib).wait_send()
        act_copy(k, opp_row, opp_row, fwd_send, fwd_recv, sib).wait_send()
        act_store(k).wait()
    store_cols.wait()
    store_kept.wait()
    store_give.wait()
    store_keep.wait()


def exchange(x_rows, dy_rows, gate, up, down):
    hbm = pl.BlockSpec(memory_space=pl.ANY)
    vmem = pl.BlockSpec(memory_space=pltpu.VMEM)
    dma = pltpu.SemaphoreType.DMA
    return pl.pallas_call(
        exchange_kernel,
        name='exchange',
        out_shape=(jax.ShapeDtypeStruct((3, 128, HID), BF16),
                   jax.ShapeDtypeStruct((2, 128, 1024), BF16),
                   jax.ShapeDtypeStruct((2, 64, 1024), F32),
                   jax.ShapeDtypeStruct((2, 64, 1024), F32),
                   jax.ShapeDtypeStruct((2, 64, 1024), BF16)),
        in_specs=[vmem, vmem, hbm, hbm, hbm],
        out_specs=(hbm,) * 5,
        scratch_shapes=[
            pltpu.VMEM((1024, HID), BF16), pltpu.VMEM((1024, HID), BF16), pltpu.VMEM((HID, 1024), BF16),
            pltpu.VMEM((3, 128, HID), F32), pltpu.VMEM((3, 64, HID), F32), pltpu.VMEM((3, 32, HID), F32),
            pltpu.VMEM((3, 128, HID), BF16), pltpu.VMEM((2, 128, 1024), BF16), pltpu.VMEM((2, 128, 1024), F32),
            dma((3, NCH)), dma((2, 3)), dma((2, 3)),
            dma((NCH,)), dma((NCH,)), dma((NCH,)), dma((NCH,)),
            dma((NCH,)), dma((NCH,)), dma((NCH,)), dma((NCH,)), dma((NCH,)), dma((NCH,)),
            dma((NCH,)), dma((2,)), dma((2,)),
        ],
        compiler_params=pltpu.CompilerParams(collective_id=0, has_side_effects=True, vmem_limit_bytes=VMEM_CAP),
        cost_estimate=pl.CostEstimate(flops=9 * 10**9, bytes_accessed=4 * 10**7, transcendentals=0),
    )(x_rows, dy_rows, gate, up, down)


def finish_kernel(keep_ref, got_ref, kept_cols_ref, y_out, dx_out, ready, landed, send_sem, recv_sem, loc_sem):
    t = lax.axis_index('tp')
    d = lax.axis_index('dp')
    cx, c = d // 2, lax.rem(d, 2)
    barrier = pltpu.get_barrier_semaphore()
    for dt in range(2):
        for dd in range(4):
            if dt or dd:
                pl.semaphore_signal(barrier, inc=1, device_id={'tp': lax.rem(t + dt, 2), 'dp': lax.rem(d + dd, 4)},
                                    device_id_type=MESH)
    total = keep_ref[...] + got_ref[...]
    ready[...] = (kept_cols_ref[...].astype(F32) + total).astype(BF16)
    pl.semaphore_wait(barrier, 7)
    block = pl.ds(pl.multiple_of(1024 * d, 128), 1024)

    def send(ocx, ot):
        chip = cx if ocx == 0 else 1 - cx
        return pltpu.make_async_remote_copy(
            src_ref=ready.at[:, pl.ds(pl.multiple_of(32 * chip, 32), 32), :],
            dst_ref=landed.at[:, :, block],
            send_sem=send_sem.at[2 * ocx + ot], recv_sem=recv_sem.at[d],
            device_id={'tp': t if ot == 0 else 1 - t, 'dp': 2 * chip + t}, device_id_type=MESH)

    def arrive(s):
        return pltpu.make_async_remote_copy(
            src_ref=ready.at[:, pl.ds(0, 32), :], dst_ref=landed.at[:, :, pl.ds(1024 * s, 1024)],
            send_sem=send_sem.at[0], recv_sem=recv_sem.at[s],
            device_id={'tp': 1 - t}, device_id_type=MESH)

    local = c == t
    for ocx, ot in ((1, 1), (1, 0), (0, 1)):
        send(ocx, ot).start()

    @pl.when(jnp.logical_not(local))
    def _():
        send(0, 0).start()

    @pl.when(local)
    def _():
        landed[:, :, block] = ready[:, pl.ds(pl.multiple_of(32 * cx, 32), 32), :]

    for s in range(4):
        @pl.when(jnp.logical_not(jnp.logical_and(local, d == s)))
        def _():
            arrive(s).wait_recv()

    stores = (pltpu.make_async_copy(landed.at[0], y_out, loc_sem.at[0]),
              pltpu.make_async_copy(landed.at[1], dx_out, loc_sem.at[1]))
    for s in stores:
        s.start()
    for ocx, ot in ((1, 1), (1, 0), (0, 1)):
        send(ocx, ot).wait_send()

    @pl.when(jnp.logical_not(local))
    def _():
        send(0, 0).wait_send()

    for s in stores:
        s.wait()


def finish(keep, got, kept_cols):
    vmem = pl.BlockSpec(memory_space=pltpu.VMEM)
    hbm = pl.BlockSpec(memory_space=pl.ANY)
    rows = jax.ShapeDtypeStruct((32, 4096), BF16)
    dma = pltpu.SemaphoreType.DMA
    return pl.pallas_call(
        finish_kernel,
        name='finish',
        out_shape=(rows, rows),
        in_specs=[vmem] * 3,
        out_specs=(hbm, hbm),
        scratch_shapes=[pltpu.VMEM((2, 64, 1024), BF16), pltpu.VMEM((2, 32, 4096), BF16),
                        dma((4,)), dma((4,)), dma((2,))],
        compiler_params=pltpu.CompilerParams(collective_id=1, has_side_effects=True),
        cost_estimate=pl.CostEstimate(flops=10**6, bytes_accessed=2 * 10**6, transcendentals=0),
    )(keep, got, kept_cols)


def grad_cols_kernel(cols_ref, act_ref, o_ref):
    o_ref[...] = lax.dot_general(cols_ref[...], act_ref[...], (((0,), (0,)), ((), ())), preferred_element_type=F32)


def grad_up(cols, act, which):
    return pl.pallas_call(
        grad_cols_kernel,
        name='grad_in',
        grid=(pl.cdiv(HID, 512),),
        out_shape=jax.ShapeDtypeStruct((1024, HID), F32),
        in_specs=[pl.BlockSpec((None, 128, 1024), lambda i: (0, 0, 0)),
                  pl.BlockSpec((None, 128, 512), lambda i: (which, 0, i))],
        out_specs=pl.BlockSpec((1024, 512), lambda i: (0, i)),
        cost_estimate=pl.CostEstimate(flops=2 * 128 * 1024 * HID, bytes_accessed=4 * 1024 * HID, transcendentals=0),
    )(cols, act)


def grad_down(cols, act):
    return pl.pallas_call(
        grad_cols_kernel,
        name='grad_out',
        grid=(pl.cdiv(HID, 512),),
        out_shape=jax.ShapeDtypeStruct((HID, 1024), F32),
        in_specs=[pl.BlockSpec((None, 128, 512), lambda i: (0, 0, i)),
                  pl.BlockSpec((None, 128, 1024), lambda i: (1, 0, 0))],
        out_specs=pl.BlockSpec((512, 1024), lambda i: (i, 0)),
        cost_estimate=pl.CostEstimate(flops=2 * 128 * 1024 * HID, bytes_accessed=4 * 1024 * HID, transcendentals=0),
    )(act, cols)


def solution(mesh):
    def device_pass(x_rows, gate_blk, up_blk, down_blk, dy_rows):
        act, cols, keep, give, kept_cols = exchange(x_rows, dy_rows, gate_blk, up_blk, down_blk)
        got = lax.ppermute(give, 'tp', [(0, 1), (1, 0)])
        dw_down = grad_down(cols, act)
        dw_gate = grad_up(cols, act, 1)
        dw_up = grad_up(cols, act, 2)
        y_rows, dx_rows = finish(keep, got, kept_cols)
        return y_rows, dx_rows, dw_gate, dw_up, dw_down

    row_spec = P('dp', None)
    weight_spec = P('dp', 'tp')
    down_spec = P('tp', 'dp')
    return jax.shard_map(device_pass, mesh=mesh,
                         in_specs=(row_spec, weight_spec, weight_spec, down_spec, row_spec),
                         out_specs=(row_spec, row_spec, weight_spec, weight_spec, down_spec),
                         check_vma=False)
```

time: 301 us -> 144 us (0.48)
  Pallas kernels: 0 us -> 136 us
  waiting for transfers between devices: 128 us -> 0.01 us
  matrix products: 77.6 us -> 0 us
  local copies, waits for them, and re-layouts: 47.9 us -> 4.13 us
  blocking collectives: 18.8 us -> 0 us
  between operations: 14.2 us -> 0.65 us
  other arithmetic: 6.39 us -> 0 us
  starting transfers between devices: 7.27 us -> 1.54 us
    pallas_call x0 -> x5, Pallas kernels: none -> 136 us  [the longest x1 90.2 us: exchange(): pl.pallas_call(exchange_kernel, name='exchange', out_shape=(jax.ShapeDtyp...]
    dot_general x9 -> x0, matrix products: 77.6 us -> none  [the longest x1 9.73 us: device_pass(): jnp.einsum('td,tf->df', x_cols, up_all, preferred_element_type=jnp.float32)]
    reduce_scatter x3 -> x0, waiting for transfers between devices: 72.7 us -> none  [the longest x1 33.1 us: device_pass(): lax.psum_scatter(gate_part, 'dp', scatter_dimension=0, tiled=True)]
    unnamed x10 -> x4, local copies, waits for them, and re-layouts: 45.5 us -> 4.13 us
    all_gather x3 -> x0, waiting for transfers between devices: 34.5 us -> none  [the longest x1 14.5 us: device_pass(): hidden_all = lax.all_gather(hidden, 'dp', axis=0, tiled=True)]
    all_to_all x2 -> x0, blocking collectives: 18.8 us -> none  [the longest x1 10.4 us: device_pass(): dy_cols = lax.all_to_all(dy_rows, 'dp', 1, 0, tiled=True)]
    psum x1 -> x0, waiting for transfers between devices: 15.5 us -> none  [device_pass(): lax.psum(out_part, 'tp')]
    all_to_all x2 -> x0, starting transfers between devices: 6.81 us -> none  [the longest x1 3.41 us: device_pass(): y_rows = lax.all_to_all(y_cols, 'dp', 0, 1, tiled=True)]
  transfers between devices with their start and end apart: 9 -> 1, of which waited for: 8 -> 0; matrix products, arithmetic and copies ran while one was open for 36% -> 0% of each run, Pallas kernels for 0% -> 25%
where the time goes in v1:
time: 144 us; the launch traced here: 143 us
  Pallas kernels  136 us (94%)
  local copies, waits for them, and re-layouts  4.13 us (3%)
  starting transfers between devices  1.54 us (1%)
    pallas_call x1, Pallas kernels, exchange(): pl.pallas_call(exchange_kernel, name='exchange', out_shape=(jax.ShapeDtyp...  90.2 us
    pallas_call x2, Pallas kernels, grad_up(): pl.pallas_call(grad_cols_kernel, name='grad_in', grid=(pl.cdiv(HID, 512),...  23.6 us
    pallas_call x1, Pallas kernels, grad_down(): pl.pallas_call(grad_cols_kernel, name='grad_out', grid=(pl.cdiv(HID, 512)...  11.8 us
    pallas_call x1, Pallas kernels, finish(): pl.pallas_call(finish_kernel, name='finish', out_shape=(rows, rows), in_s...  10.8 us
    unnamed x4, local copies, waits for them, and re-layouts  4.13 us
  transfers between devices with their start and end apart: 1, of which 0 were waited for; matrix products, arithmetic and copies ran while one was open for 0% of the time, Pallas kernels for 25%

profile of v1, /device:TPU:0, one launch (start us, length us, event | category | flops | bytes accessed | tf_op | source)
XLA Modules:
  0.0 142.7 jit_solution(13502414167933629178)
XLA Ops:
  0.6 90.2 %exchange.1 = (bf16[3,128,5504]{2,1,0:T(8,128)(2,1)}, bf16[2,128,1024]{2,1,0:T(8,128)(2,1)}, f32[2,64,1024]{2,1,0:T(8,128)}, f32[2,64,1024]{2,1,0:T(8,128)}, bf16[2,64,1024]{2,1,0:T(8,128)(2,1)}) custom-call(bf16[32,4096]{1,0:T(8,128)(2,1)} %x_ref.1, bf16[32,4096]{1,0:T(8,128)(2,1)} %dy_ref.1, bf16[1024,5504]{1,0:T(8,128)(2,1)} %wg_hbm.1, ...), custom_call_target="tpu_custom_call" | custom-call | flops 8999999488 | bytes 40000000 | tf_op jit(solution)/shard_map/exchange/pallas_call | solution.py:235
  90.8 1.5 %collective-permute-start = (f32[2,64,1024]{2,1,0:T(8,128)}, f32[2,64,1024]{2,1,0:T(8,128)S(1)}, u32[]{:S(2)}, u32[]{:S(2)}) collective-permute-start(f32[2,64,1024]{2,1,0:T(8,128)} %get-tuple-element.13), channel_id=1, source_target_pairs={{0,4},{4,0},{1,5},{5,1},{2,6},{6,2},{3,7},{7,3}} | collective-permute-start | bytes 1572872 | tf_op jit(solution)/shard_map/ppermute | solution.py:371
  92.4 11.8 %grad_out.1 = f32[5504,1024]{1,0:T(8,128)} custom-call(bf16[3,128,5504]{2,1,0:T(8,128)(2,1)} %get-tuple-element.18.act_ref.cols_ref, bf16[2,128,1024]{2,1,0:T(8,128)(2,1)} %get-tuple-element.17.cols_ref.act_ref), custom_call_target="tpu_custom_call" | custom-call | flops 1442840576 | bytes 22544384 | tf_op jit(solution)/shard_map/grad_out/pallas_call | solution.py:356
  104.2 11.8 %grad_in.3 = f32[1024,5504]{1,0:T(8,128)} custom-call(bf16[2,128,1024]{2,1,0:T(8,128)(2,1)} %get-tuple-element.17.cols_ref.act_ref, bf16[3,128,5504]{2,1,0:T(8,128)(2,1)} %get-tuple-element.18.act_ref.cols_ref), custom_call_target="tpu_custom_call" | custom-call | flops 1442840576 | bytes 22544384 | tf_op jit(solution)/shard_map/grad_in/pallas_call | solution.py:343
  116.0 11.8 %grad_in.2 = f32[1024,5504]{1,0:T(8,128)} custom-call(bf16[2,128,1024]{2,1,0:T(8,128)(2,1)} %get-tuple-element.17.cols_ref.act_ref, bf16[3,128,5504]{2,1,0:T(8,128)(2,1)} %get-tuple-element.18.act_ref.cols_ref), custom_call_target="tpu_custom_call" | custom-call | flops 1442840576 | bytes 22544384 | tf_op jit(solution)/shard_map/grad_in/pallas_call | solution.py:343
  127.8 0.0 collective-permute-done.got_ref
  127.8 0.0 copy-start
  127.8 0.8 copy-done
  128.6 10.8 %finish.1 = (bf16[32,4096]{1,0:T(8,128)(2,1)}, bf16[32,4096]{1,0:T(8,128)(2,1)}) custom-call(f32[2,64,1024]{2,1,0:T(8,128)} %get-tuple-element.12.keep_ref, f32[2,64,1024]{2,1,0:T(8,128)} %copy-done, bf16[2,64,1024]{2,1,0:T(8,128)(2,1)} %get-tuple-element.14.kept_cols_ref), custom_call_target="tpu_custom_call" | custom-call | flops 1000000 | bytes 2000000 | tf_op jit(solution)/shard_map/finish/pallas_call | solution.py:325
  139.4 1.7 %copy.12 = bf16[32,4096]{1,0:T(8,128)(2,1)} copy(bf16[32,4096]{1,0:T(8,128)(2,1)} %get-tuple-element.24) | data formatting | bytes 524288
  141.1 1.7 %copy.13 = bf16[32,4096]{1,0:T(8,128)(2,1)} copy(bf16[32,4096]{1,0:T(8,128)(2,1)} %get-tuple-element.25) | data formatting | bytes 524288
Async XLA Ops:
  90.8 37.0 %collective-permute-start = (f32[2,64,1024]{2,1,0:T(8,128)}, f32[2,64,1024]{2,1,0:T(8,128)S(1)}, u32[]{:S(2)}, u32[]{:S(2)}) collective-permute-start(f32[2,64,1024]{2,1,0:T(8,128)} %get-tuple-element.13), channel_id=1, source_target_pairs={{0,4},{4,0},{1,5},{5,1},{2,6},{6,2},{3,7},{7,3}} | collective-permute-start | bytes 1572872 | tf_op jit(solution)/shard_map/ppermute | solution.py:371
  127.8 0.8 copy-start

commit v2 on v1

--- a/solution.py
+++ b/solution.py
@@ -29,10 +29,10 @@
 
 
 def exchange_kernel(x_ref, dy_ref, wg_hbm, wu_hbm, wd_hbm,
-                    act_out, cols_out, keep_out, give_out, kept_cols_out,
-                    wg, wu, wd, part, from_sib, from_opp, act, cols, acc,
+                    act_out, act_t_out, cols_t_out, dy_cols_out, keep_out, give_out, kept_cols_out,
+                    wg, wu, wd, part, from_sib, from_opp, act, act_t, cols, cols_t, acc,
                     w_sem, x_send, x_recv, s1_send, s1_recv, s2_send, s2_recv,
-                    sib_send, sib_recv, opp_send, opp_recv, fwd_send, fwd_recv, out_sem, col_sem, acc_sem):
+                    sib_send, sib_recv, opp_send, opp_recv, fwd_send, fwd_recv, out_sem, out_t_sem, col_sem, acc_sem):
     t = lax.axis_index('tp')
     d = lax.axis_index('dp')
     cx, c = d // 2, lax.rem(d, 2)
@@ -166,13 +166,21 @@
 
     def act_store(k):
         cs = pl.ds(STARTS[k], WIDTHS[k])
-        return pltpu.make_async_copy(act.at[:, :, cs], act_out.at[:, :, cs], out_sem.at[k])
+        return (pltpu.make_async_copy(act.at[pl.ds(1, 2), :, cs], act_out.at[:, :, cs], out_sem.at[k]),
+                pltpu.make_async_copy(act_t.at[cs, :], act_t_out.at[cs, :], out_t_sem.at[k]))
 
     def outputs(k):
         act_copy(k, own_row, sib_row, sib_send, sib_recv, sib).wait_recv()
         act_copy(k, opp_row, far_row, fwd_send, fwd_recv, sib).wait_recv()
-        act_store(k).start()
         cs = pl.ds(STARTS[k], WIDTHS[k])
+
+        def flip(col, width):
+            ts = pl.ds(col, width)
+            act_t[ts, :] = act[0, :, ts].T
+
+        column_tiles(STARTS[k], WIDTHS[k], flip)
+        for copy in act_store(k):
+            copy.start()
 
         def step(n, carry):
             ns = pl.ds(pl.multiple_of(n * 256, 256), 256)
@@ -192,11 +200,16 @@
     for k in range(NCH):
         partials(k)
         if k == 0:
-            store_cols = pltpu.make_async_copy(cols, cols_out, col_sem.at[0])
-            store_cols.start()
+            store_dy = pltpu.make_async_copy(cols.at[1], dy_cols_out, col_sem.at[0])
+            store_dy.start()
             store_kept = pltpu.make_async_copy(cols.at[:, pl.ds(pl.multiple_of(64 * t, 64), 64), :],
                                                kept_cols_out, col_sem.at[1])
             store_kept.start()
+        if k == 1:
+            for n in range(4):
+                cols_t[n * 256:(n + 1) * 256, :] = cols[0, :, n * 256:(n + 1) * 256].T
+            store_cols_t = pltpu.make_async_copy(cols_t, cols_t_out, col_sem.at[2])
+            store_cols_t.start()
         if k >= 1:
             chip_sum(k - 1)
     chip_sum(NCH - 1)
@@ -221,8 +234,10 @@
         act_copy(k, own_row, own_row, opp_send, opp_recv, opp).wait_send()
         act_copy(k, own_row, own_row, sib_send, sib_recv, sib).wait_send()
         act_copy(k, opp_row, opp_row, fwd_send, fwd_recv, sib).wait_send()
-        act_store(k).wait()
-    store_cols.wait()
+        for copy in act_store(k):
+            copy.wait()
+    store_dy.wait()
+    store_cols_t.wait()
     store_kept.wait()
     store_give.wait()
     store_keep.wait()
@@ -235,21 +250,24 @@
     return pl.pallas_call(
         exchange_kernel,
         name='exchange',
-        out_shape=(jax.ShapeDtypeStruct((3, 128, HID), BF16),
-                   jax.ShapeDtypeStruct((2, 128, 1024), BF16),
+        out_shape=(jax.ShapeDtypeStruct((2, 128, HID), BF16),
+                   jax.ShapeDtypeStruct((HID, 128), BF16),
+                   jax.ShapeDtypeStruct((1024, 128), BF16),
+                   jax.ShapeDtypeStruct((128, 1024), BF16),
                    jax.ShapeDtypeStruct((2, 64, 1024), F32),
                    jax.ShapeDtypeStruct((2, 64, 1024), F32),
                    jax.ShapeDtypeStruct((2, 64, 1024), BF16)),
         in_specs=[vmem, vmem, hbm, hbm, hbm],
-        out_specs=(hbm,) * 5,
+        out_specs=(hbm,) * 7,
         scratch_shapes=[
             pltpu.VMEM((1024, HID), BF16), pltpu.VMEM((1024, HID), BF16), pltpu.VMEM((HID, 1024), BF16),
             pltpu.VMEM((3, 128, HID), F32), pltpu.VMEM((3, 64, HID), F32), pltpu.VMEM((3, 32, HID), F32),
-            pltpu.VMEM((3, 128, HID), BF16), pltpu.VMEM((2, 128, 1024), BF16), pltpu.VMEM((2, 128, 1024), F32),
+            pltpu.VMEM((3, 128, HID), BF16), pltpu.VMEM((HID, 128), BF16), pltpu.VMEM((2, 128, 1024), BF16),
+            pltpu.VMEM((1024, 128), BF16), pltpu.VMEM((2, 128, 1024), F32),
             dma((3, NCH)), dma((2, 3)), dma((2, 3)),
             dma((NCH,)), dma((NCH,)), dma((NCH,)), dma((NCH,)),
             dma((NCH,)), dma((NCH,)), dma((NCH,)), dma((NCH,)), dma((NCH,)), dma((NCH,)),
-            dma((NCH,)), dma((2,)), dma((2,)),
+            dma((NCH,)), dma((NCH,)), dma((3,)), dma((2,)),
         ],
         compiler_params=pltpu.CompilerParams(collective_id=0, has_side_effects=True, vmem_limit_bytes=VMEM_CAP),
         cost_estimate=pl.CostEstimate(flops=9 * 10**9, bytes_accessed=4 * 10**7, transcendentals=0),
@@ -335,44 +353,142 @@
     )(keep, got, kept_cols)
 
 
-def grad_cols_kernel(cols_ref, act_ref, o_ref):
-    o_ref[...] = lax.dot_general(cols_ref[...], act_ref[...], (((0,), (0,)), ((), ())), preferred_element_type=F32)
-
-
-def grad_up(cols, act, which):
+TILE = 512
+TILES = HID // TILE
+LAST = HID - TILES * TILE
+SLOTS = 6
+
+
+def stream_tiles(compute, store):
+    def step(i, carry):
+        slot = lax.rem(i, SLOTS)
+
+        @pl.when(i >= SLOTS)
+        def _():
+            store(i - SLOTS, slot, TILE).wait()
+
+        compute(i, slot, TILE)
+        store(i, slot, TILE).start()
+        return carry
+
+    lax.fori_loop(0, TILES, step, 0)
+    store(TILES - SLOTS, TILES % SLOTS, TILE).wait()
+    compute(TILES, TILES % SLOTS, LAST)
+    store(TILES, TILES % SLOTS, LAST).start()
+
+
+def drain_tiles(store):
+    for i in range(TILES - SLOTS + 1, TILES):
+        store(i, i % SLOTS, TILE).wait()
+    store(TILES, TILES % SLOTS, LAST).wait()
+
+
+def tile_slice(i, width):
+    return pl.ds(pl.multiple_of(i * TILE, 128), width)
+
+
+def column_job(left, right, ring, out, sem):
+    def compute(i, slot, width):
+        ring[slot, :, pl.ds(0, width)] = jnp.dot(left[...], right[:, tile_slice(i, width)],
+                                                 preferred_element_type=F32)
+
+    def store(i, slot, width):
+        return pltpu.make_async_copy(ring.at[slot, :, pl.ds(0, width)], out.at[:, tile_slice(i, width)], sem.at[slot])
+
+    return compute, store
+
+
+def row_job(left, right, ring, out, sem):
+    def compute(i, slot, width):
+        ring[slot, pl.ds(0, width), :] = jnp.dot(left[tile_slice(i, width), :], right[...],
+                                                 preferred_element_type=F32)
+
+    def store(i, slot, width):
+        return pltpu.make_async_copy(ring.at[slot, pl.ds(0, width), :], out.at[tile_slice(i, width), :], sem.at[slot])
+
+    return compute, store
+
+
+def grads_first_kernel(act_t_hbm, dy_cols_hbm, cols_t_hbm, act_hbm, down_out, gate_out,
+                       act_t, dy_cols, cols_t, act, ring_a, ring_b, in_sem, sem_a, sem_b):
+    loads = [pltpu.make_async_copy(src, dst, in_sem.at[n]) for n, (src, dst) in enumerate((
+        (dy_cols_hbm, dy_cols), (act_t_hbm, act_t), (cols_t_hbm, cols_t), (act_hbm.at[0], act)))]
+    for load in loads:
+        load.start()
+    loads[0].wait()
+    loads[1].wait()
+    compute, store = row_job(act_t, dy_cols, ring_a, down_out, sem_a)
+    stream_tiles(compute, store)
+    loads[2].wait()
+    loads[3].wait()
+    compute_b, store_b = column_job(cols_t, act, ring_b, gate_out, sem_b)
+    stream_tiles(compute_b, store_b)
+    drain_tiles(store)
+    drain_tiles(store_b)
+
+
+def grads_first(act_t, dy_cols, cols_t, act):
+    hbm = pl.BlockSpec(memory_space=pl.ANY)
+    dma = pltpu.SemaphoreType.DMA
     return pl.pallas_call(
-        grad_cols_kernel,
-        name='grad_in',
-        grid=(pl.cdiv(HID, 512),),
-        out_shape=jax.ShapeDtypeStruct((1024, HID), F32),
-        in_specs=[pl.BlockSpec((None, 128, 1024), lambda i: (0, 0, 0)),
-                  pl.BlockSpec((None, 128, 512), lambda i: (which, 0, i))],
-        out_specs=pl.BlockSpec((1024, 512), lambda i: (0, i)),
+        grads_first_kernel,
+        name='grads_first',
+        out_shape=(jax.ShapeDtypeStruct((HID, 1024), F32), jax.ShapeDtypeStruct((1024, HID), F32)),
+        in_specs=[hbm] * 4,
+        out_specs=(hbm, hbm),
+        scratch_shapes=[pltpu.VMEM((HID, 128), BF16), pltpu.VMEM((128, 1024), BF16), pltpu.VMEM((1024, 128), BF16),
+                        pltpu.VMEM((128, HID), BF16), pltpu.VMEM((SLOTS, TILE, 1024), F32),
+                        pltpu.VMEM((SLOTS, 1024, TILE), F32), dma((4,)), dma((SLOTS,)), dma((SLOTS,))],
+        compiler_params=pltpu.CompilerParams(vmem_limit_bytes=VMEM_CAP),
+        cost_estimate=pl.CostEstimate(flops=4 * 128 * 1024 * HID, bytes_accessed=8 * 1024 * HID, transcendentals=0),
+    )(act_t, dy_cols, cols_t, act)
+
+
+def grads_last_kernel(cols_t_hbm, act_hbm, y_hbm, dx_hbm, up_out, y_out, dx_out,
+                      cols_t, act, rows, ring, in_sem, sem, row_sem):
+    loads = [pltpu.make_async_copy(src, dst, in_sem.at[n]) for n, (src, dst) in enumerate((
+        (cols_t_hbm, cols_t), (act_hbm.at[1], act), (y_hbm, rows.at[0]), (dx_hbm, rows.at[1])))]
+    for load in loads:
+        load.start()
+    loads[0].wait()
+    loads[1].wait()
+    compute, store = column_job(cols_t, act, ring, up_out, sem)
+    stream_tiles(compute, store)
+    loads[2].wait()
+    loads[3].wait()
+    copies = (pltpu.make_async_copy(rows.at[0], y_out, row_sem.at[0]),
+              pltpu.make_async_copy(rows.at[1], dx_out, row_sem.at[1]))
+    for copy in copies:
+        copy.start()
+    drain_tiles(store)
+    for copy in copies:
+        copy.wait()
+
+
+def grads_last(cols_t, act, y, dx):
+    hbm = pl.BlockSpec(memory_space=pl.ANY)
+    dma = pltpu.SemaphoreType.DMA
+    rows = jax.ShapeDtypeStruct((32, 4096), BF16)
+    return pl.pallas_call(
+        grads_last_kernel,
+        name='grads_last',
+        out_shape=(jax.ShapeDtypeStruct((1024, HID), F32), rows, rows),
+        in_specs=[hbm] * 4,
+        out_specs=(hbm, hbm, hbm),
+        scratch_shapes=[pltpu.VMEM((1024, 128), BF16), pltpu.VMEM((128, HID), BF16), pltpu.VMEM((2, 32, 4096), BF16),
+                        pltpu.VMEM((SLOTS, 1024, TILE), F32), dma((4,)), dma((SLOTS,)), dma((2,))],
+        compiler_params=pltpu.CompilerParams(vmem_limit_bytes=VMEM_CAP),
         cost_estimate=pl.CostEstimate(flops=2 * 128 * 1024 * HID, bytes_accessed=4 * 1024 * HID, transcendentals=0),
-    )(cols, act)
-
-
-def grad_down(cols, act):
-    return pl.pallas_call(
-        grad_cols_kernel,
-        name='grad_out',
-        grid=(pl.cdiv(HID, 512),),
-        out_shape=jax.ShapeDtypeStruct((HID, 1024), F32),
-        in_specs=[pl.BlockSpec((None, 128, 512), lambda i: (0, 0, i)),
-                  pl.BlockSpec((None, 128, 1024), lambda i: (1, 0, 0))],
-        out_specs=pl.BlockSpec((512, 1024), lambda i: (i, 0)),
-        cost_estimate=pl.CostEstimate(flops=2 * 128 * 1024 * HID, bytes_accessed=4 * 1024 * HID, transcendentals=0),
-    )(act, cols)
+    )(cols_t, act, y, dx)
 
 
 def solution(mesh):
     def device_pass(x_rows, gate_blk, up_blk, down_blk, dy_rows):
-        act, cols, keep, give, kept_cols = exchange(x_rows, dy_rows, gate_blk, up_blk, down_blk)
+        act, act_t, cols_t, dy_cols, keep, give, kept_cols = exchange(x_rows, dy_rows, gate_blk, up_blk, down_blk)
         got = lax.ppermute(give, 'tp', [(0, 1), (1, 0)])
-        dw_down = grad_down(cols, act)
-        dw_gate = grad_up(cols, act, 1)
-        dw_up = grad_up(cols, act, 2)
-        y_rows, dx_rows = finish(keep, got, kept_cols)
+        dw_down, dw_gate = grads_first(act_t, dy_cols, cols_t, act)
+        y_part, dx_part = finish(keep, got, kept_cols)
+        dw_up, y_rows, dx_rows = grads_last(cols_t, act, y_part, dx_part)
         return y_rows, dx_rows, dw_gate, dw_up, dw_down
 
     row_spec = P('dp', None)

time: 144 us -> 130 us (0.903)
  Pallas kernels: 136 us -> 128 us
  local copies, waits for them, and re-layouts: 4.13 us -> 0 us
    pallas_call x3 -> x2, Pallas kernels: 35.5 us -> 26 us  [the longest x1 16.3 us: grads_first(): pl.pallas_call(grads_first_kernel, name='grads_first', out_shape=(jax.Sha...]
    unnamed x4 -> x0, local copies, waits for them, and re-layouts: 4.13 us -> none
  transfers between devices with their start and end apart: 1 -> 1, of which waited for: 0 -> 0; matrix products, arithmetic and copies ran while one was open for 0% -> 0% of each run, Pallas kernels for 25% -> 13%
where the time goes in v2:
time: 130 us
  Pallas kernels  128 us (98%)
  starting transfers between devices  1.54 us (1%)
    pallas_call x1, Pallas kernels, exchange(): pl.pallas_call(exchange_kernel, name='exchange', out_shape=(jax.ShapeDtyp...  91 us
    pallas_call x1, Pallas kernels, grads_first(): pl.pallas_call(grads_first_kernel, name='grads_first', out_shape=(jax.Sha...  16.3 us
    pallas_call x1, Pallas kernels, finish(): pl.pallas_call(finish_kernel, name='finish', out_shape=(rows, rows), in_s...  10.8 us
    pallas_call x1, Pallas kernels, grads_last(): pl.pallas_call(grads_last_kernel, name='grads_last', out_shape=(jax.Shape...  9.64 us
  transfers between devices with their start and end apart: 1, of which 0 were waited for; matrix products, arithmetic and copies ran while one was open for 0% of the time, Pallas kernels for 13%

profile of v2, /device:TPU:0, one launch (start us, length us, event | category | flops | bytes accessed | tf_op | source)
XLA Modules:
  0.0 130.0 jit_solution(9844719173193397260)
XLA Ops:
  0.6 91.0 %exchange.1 = (bf16[2,128,5504]{2,1,0:T(8,128)(2,1)}, bf16[5504,128]{1,0:T(8,128)(2,1)}, bf16[1024,128]{1,0:T(8,128)(2,1)}, bf16[128,1024]{1,0:T(8,128)(2,1)}, f...) custom-call(bf16[32,4096]{1,0:T(8,128)(2,1)} %x_ref.1, bf16[32,4096]{1,0:T(8,128)(2,1)} %dy_ref.1, ...), custom_call_target="tpu_custom_call" | custom-call | flops 8999999488 | bytes 40000000 | tf_op jit(solution)/shard_map/exchange/pallas_call | solution.py:250
  91.7 1.5 %collective-permute-start = (f32[2,64,1024]{2,1,0:T(8,128)}, f32[2,64,1024]{2,1,0:T(8,128)}, u32[]{:S(2)}, u32[]{:S(2)}) collective-permute-start(f32[2,64,1024]{2,1,0:T(8,128)} %get-tuple-element.22), channel_id=1, source_target_pairs={{0,4},{4,0},{1,5},{5,1},{2,6},{6,2},{3,7},{7,3}} | collective-permute-start | bytes 1572872 | tf_op jit(solution)/shard_map/ppermute | solution.py:488
  93.2 16.3 %grads_first.1 = (f32[5504,1024]{1,0:T(8,128)}, f32[1024,5504]{1,0:T(8,128)}) custom-call(bf16[5504,128]{1,0:T(8,128)(2,1)} %get-tuple-element.28.act_t_hbm, bf16[128,1024]{1,0:T(8,128)(2,1)} %get-tuple-element.29.dy_cols_hbm, bf16[1024,128]{1,0:T(8,128)(2,1)} %get-tuple-element.19.cols_t_hbm, bf16[2,128,5504]{2,1,0:T(8,128)(2,1)} %get-tuple-element.20.act_hbm), custom_call_target="tpu_custom_call" | custom-call | flops 2885681152 | bytes 45088768 | tf_op jit(solution)/shard_map/grads_first/pallas_call | solution.py:433
  109.6 0.0 collective-permute-done.got_ref
  109.6 10.8 %finish.1 = (bf16[32,4096]{1,0:T(8,128)(2,1)}, bf16[32,4096]{1,0:T(8,128)(2,1)}) custom-call(f32[2,64,1024]{2,1,0:T(8,128)} %get-tuple-element.21.keep_ref, f32[2,64,1024]{2,1,0:T(8,128)} %collective-permute-done.got_ref, bf16[2,64,1024]{2,1,0:T(8,128)(2,1)} %get-tuple-element.23.kept_cols_ref), custom_call_target="tpu_custom_call" | custom-call | flops 1000000 | bytes 2000000 | tf_op jit(solution)/shard_map/finish/pallas_call | solution.py:343
  120.3 9.6 %grads_last.1 = (f32[1024,5504]{1,0:T(8,128)}, bf16[32,4096]{1,0:T(8,128)(2,1)}, bf16[32,4096]{1,0:T(8,128)(2,1)}) custom-call(bf16[1024,128]{1,0:T(8,128)(2,1)} %get-tuple-element.19.cols_t_hbm, bf16[2,128,5504]{2,1,0:T(8,128)(2,1)} %get-tuple-element.20.act_hbm, bf16[32,4096]{1,0:T(8,128)(2,1)} %get-tuple-element.24.y_hbm, ...), custom_call_target="tpu_custom_call" | custom-call | flops 1442840576 | bytes 22544384 | tf_op jit(solution)/shard_map/grads_last/pallas_call | solution.py:472
Async XLA Ops:
  91.7 17.9 %collective-permute-start = (f32[2,64,1024]{2,1,0:T(8,128)}, f32[2,64,1024]{2,1,0:T(8,128)}, u32[]{:S(2)}, u32[]{:S(2)}) collective-permute-start(f32[2,64,1024]{2,1,0:T(8,128)} %get-tuple-element.22), channel_id=1, source_target_pairs={{0,4},{4,0},{1,5},{5,1},{2,6},{6,2},{3,7},{7,3}} | collective-permute-start | bytes 1572872 | tf_op jit(solution)/shard_map/ppermute | solution.py:488

commit v3 on v0

v3 whole, which is shorter than its diff:
```python
import jax
import jax.numpy as jnp
from jax import lax
from jax.experimental import pallas as pl
from jax.experimental.pallas import tpu as pltpu
from jax.sharding import PartitionSpec as P

MESH = pl.DeviceIdType.MESH
F32, BF16 = jnp.float32, jnp.bfloat16
VMEM_CAP = 67043328
HID = 5504


def chunks(start, widths):
    out = []
    for w in widths:
        out.append((start, w))
        start += w
    return tuple(out)


AB = chunks(0, (512, 512, 1024, 1024, 1024, 1024, 384))
GG = chunks(0, (1024, 1024, 1024, 1024, 768, 384, 256))
NA, NG = len(AB), len(GG)
NT = 4
TW = 1024 // NT
MW = 512


def aligned(v, m):
    return pl.multiple_of(v, m)


def cols_of(chunk):
    return pl.ds(chunk[0], chunk[1])


def column_tiles(chunk, body, tile=256):
    start, width = chunk
    full = width // tile

    def step(i, carry):
        body(aligned(start + i * tile, 128), tile)
        return carry

    lax.fori_loop(0, full, step, 0)
    if width % tile:
        body(start + full * tile, width % tile)


def dot_nt(a, b):
    return lax.dot_general(a, b, (((1,), (1,)), ((), ())), preferred_element_type=F32)


def dot_nn(a, b):
    return jnp.dot(a, b, preferred_element_type=F32)


class Place:
    def __init__(self):
        self.t = lax.axis_index('tp')
        self.d = lax.axis_index('dp')
        self.cx, self.c = self.d // 2, lax.rem(self.d, 2)
        cx, c = self.cx, self.c
        self.sib = 2 * cx + (1 - c)
        self.opp = 2 * (1 - cx) + c
        self.far = 2 * (1 - cx) + (1 - c)
        self.own_row = aligned(32 * (2 * c + cx), 32)
        self.opp_row = aligned(32 * (2 * c + 1 - cx), 32)
        self.sib_row = aligned(32 * (2 * (1 - c) + cx), 32)
        self.far_row = aligned(32 * (2 * (1 - c) + 1 - cx), 32)
        self.keep = pl.ds(aligned(64 * self.t, 64), 64)
        self.give = pl.ds(aligned(64 * (1 - self.t), 64), 64)

    def enter(self):
        barrier = pltpu.get_barrier_semaphore()
        for dt in range(2):
            for dd in range(4):
                if dt or dd:
                    pl.semaphore_signal(barrier, inc=1, device_id_type=MESH, device_id={
                        'tp': lax.rem(self.t + dt, 2), 'dp': lax.rem(self.d + dd, 4)})
        return barrier


class Gather:
    def __init__(self, at, buf, parts, chunk_list, sems):
        self.at, self.buf, self.parts, self.chunks = at, buf, parts, chunk_list
        self.opp_s, self.opp_r, self.sib_s, self.sib_r, self.fwd_s, self.fwd_r = sems

    def copy(self, k, src_row, dst_row, send, recv, to):
        cs = cols_of(self.chunks[k])
        return pltpu.make_async_remote_copy(
            src_ref=self.buf.at[self.parts, pl.ds(src_row, 32), cs],
            dst_ref=self.buf.at[self.parts, pl.ds(dst_row, 32), cs],
            send_sem=send.at[k], recv_sem=recv.at[k], device_id={'dp': to}, device_id_type=MESH)

    def out_opp(self, k, dst=None):
        at = self.at
        return self.copy(k, at.own_row, at.own_row if dst is None else dst, self.opp_s, self.opp_r, at.opp)

    def out_sib(self, k, dst=None):
        at = self.at
        return self.copy(k, at.own_row, at.own_row if dst is None else dst, self.sib_s, self.sib_r, at.sib)

    def out_fwd(self, k, dst=None):
        at = self.at
        return self.copy(k, at.opp_row, at.opp_row if dst is None else dst, self.fwd_s, self.fwd_r, at.sib)

    def send(self, k):
        self.out_opp(k).start()
        self.out_sib(k).start()

    def forward(self, k):
        self.out_opp(k, self.at.opp_row).wait_recv()
        self.out_fwd(k).start()

    def arrived(self, k):
        self.out_sib(k, self.at.sib_row).wait_recv()
        self.out_fwd(k, self.at.far_row).wait_recv()

    def drain(self):
        for k in range(len(self.chunks)):
            self.out_opp(k).wait_send()
            self.out_sib(k).wait_send()
            self.out_fwd(k).wait_send()


class RowSum:
    def __init__(self, at, acc, kept, got, ready, landed, sems):
        self.at, self.acc, self.kept, self.got, self.ready, self.landed = at, acc, kept, got, ready, landed
        self.sum_s, self.sum_r, self.row_s, self.row_r = sems
        self.local = at.c == at.t

    def tile(self, n):
        return pl.ds(n * TW, TW)

    def swap(self, n):
        at = self.at
        return pltpu.make_async_remote_copy(
            src_ref=self.acc.at[at.give, self.tile(n)], dst_ref=self.got.at[:, self.tile(n)],
            send_sem=self.sum_s.at[n], recv_sem=self.sum_r.at[n], device_id={'tp': 1 - at.t}, device_id_type=MESH)

    def row_copy(self, n, ox, ot):
        at = self.at
        chip = 1 - at.cx if ox else at.cx
        return pltpu.make_async_remote_copy(
            src_ref=self.ready.at[pl.ds(aligned(32 * chip, 32), 32), self.tile(n)],
            dst_ref=self.landed.at[:, pl.ds(aligned(1024 * at.d + n * TW, 128), TW)],
            send_sem=self.row_s.at[n, 2 * ox + ot], recv_sem=self.row_r.at[n, at.d],
            device_id={'tp': 1 - at.t if ot else at.t, 'dp': 2 * chip + at.t}, device_id_type=MESH)

    def row_arrive(self, n, s):
        return pltpu.make_async_remote_copy(
            src_ref=self.ready.at[pl.ds(0, 32), self.tile(n)],
            dst_ref=self.landed.at[:, pl.ds(1024 * s + n * TW, TW)],
            send_sem=self.row_s.at[n, 0], recv_sem=self.row_r.at[n, s],
            device_id={'tp': 1 - self.at.t}, device_id_type=MESH)

    def finish(self, n):
        at, ns = self.at, self.tile(n)
        self.swap(n).wait_recv()
        total = self.acc[at.keep, ns] + self.got[:, ns]
        self.ready[:, ns] = (self.kept[at.keep, ns].astype(F32) + total).astype(BF16)
        for ox, ot in ((1, 1), (1, 0), (0, 1)):
            self.row_copy(n, ox, ot).start()

        @pl.when(jnp.logical_not(self.local))
        def _():
            self.row_copy(n, 0, 0).start()

        @pl.when(self.local)
        def _():
            self.landed[:, pl.ds(aligned(1024 * at.d + n * TW, 128), TW)] = (
                self.ready[pl.ds(aligned(32 * at.cx, 32), 32), ns])

    def collect(self):
        for n in range(NT):
            for s in range(4):
                @pl.when(jnp.logical_not(jnp.logical_and(self.local, self.at.d == s)))
                def _():
                    self.row_arrive(n, s).wait_recv()

    def drain(self):
        for n in range(NT):
            self.swap(n).wait_send()
            for ox, ot in ((1, 1), (1, 0), (0, 1)):
                self.row_copy(n, ox, ot).wait_send()

        @pl.when(jnp.logical_not(self.local))
        def _():
            for n in range(NT):
                self.row_copy(n, 0, 0).wait_send()


def gate_grads(act, slot, own, cs, a, b, g):
    s = jax.nn.sigmoid(a)
    act[slot, own, cs] = (g * b * s * (1.0 + a * (1.0 - s))).astype(BF16)
    act[slot + 1, own, cs] = (g * (a * s)).astype(BF16)


def add_dx(acc, act, slot, wg, wu, cs, fresh):
    @pl.loop(0, 1024 // MW)
    def _(n):
        ns = pl.ds(aligned(n * MW, 128), MW)
        dx = dot_nt(act[slot, :, cs], wg[ns, cs]) + dot_nt(act[slot + 1, :, cs], wu[ns, cs])
        acc[:, ns] = dx if fresh else acc[:, ns] + dx


def front_kernel(x_hbm, dy_hbm, wg_hbm, wu_hbm, wd_hbm,
                 act_out, act_t_out, cols_t_out, dy_cols_out, y_out, dx_out,
                 x_ref, dy_ref, wg, wu, wd, part, from_sib, from_opp, act, act_t, cols, cols_t, y_acc, dx_acc, y_got, y_ready, y_rows,
                 in_sem, gu_sem, d_sem, x_send, x_recv, a1_s, a1_r, a2_s, a2_r, g1_s, g1_r, g2_s, g2_r,
                 h_sems, q_sems, sum_s, sum_r, row_s, row_r, t_sem, q_sem, o_sem, dx_sem):
    at = Place()
    own, opp = pl.ds(at.own_row, 32), pl.ds(at.opp_row, 32)
    sib_half = pl.ds(aligned(64 * (1 - at.c), 64), 64)
    mine, theirs = pl.ds(aligned(32 * at.cx, 32), 32), pl.ds(aligned(32 * (1 - at.cx), 32), 32)

    def gate_up_loads(k):
        cs = cols_of(AB[k])
        return (pltpu.make_async_copy(wg_hbm.at[:, cs], wg.at[:, cs], gu_sem.at[0, k]),
                pltpu.make_async_copy(wu_hbm.at[:, cs], wu.at[:, cs], gu_sem.at[1, k]))

    def down_load(k):
        cs = cols_of(GG[k])
        return pltpu.make_async_copy(wd_hbm.at[cs, :], wd.at[cs, :], d_sem.at[k])

    barrier = at.enter()
    token_loads = (pltpu.make_async_copy(x_hbm, x_ref, in_sem.at[0]),
                   pltpu.make_async_copy(dy_hbm, dy_ref, in_sem.at[1]))
    for load in token_loads:
        load.start()
    for k in range(2):
        for load in gate_up_loads(k):
            load.start()
    pl.semaphore_wait(barrier, 7)

    peers = (at.sib, at.opp, at.far)
    tokens = (x_ref, dy_ref)

    def token_copy(i, q, row):
        return pltpu.make_async_remote_copy(
            src_ref=tokens[i].at[:, pl.ds(aligned(1024 * peers[q], 128), 1024)],
            dst_ref=cols.at[i, pl.ds(row, 32), :],
            send_sem=x_send.at[i, q], recv_sem=x_recv.at[i, q],
            device_id={'dp': peers[q]}, device_id_type=MESH)

    for i in range(2):
        token_loads[i].wait()
        for q in (2, 1, 0):
            token_copy(i, q, at.own_row).start()
    for k in range(2, NA):
        for load in gate_up_loads(k):
            load.start()
    for k in range(NG):
        down_load(k).start()
    for i in range(2):
        cols[i, own, :] = tokens[i][:, pl.ds(aligned(1024 * at.d, 128), 1024)]

    def token_wait(i):
        for q, row in enumerate((at.sib_row, at.opp_row, at.far_row)):
            token_copy(i, q, row).wait_recv()

    def core_copy(parts, chunk, k, send, recv):
        cs = cols_of(chunk)
        return pltpu.make_async_remote_copy(
            src_ref=part.at[parts, sib_half, cs], dst_ref=from_sib.at[parts, :, cs],
            send_sem=send.at[k], recv_sem=recv.at[k], device_id={'dp': at.sib}, device_id_type=MESH)

    def chip_copy(parts, chunk, k, send, recv):
        cs = cols_of(chunk)
        return pltpu.make_async_remote_copy(
            src_ref=part.at[parts, opp, cs], dst_ref=from_opp.at[parts, :, cs],
            send_sem=send.at[k], recv_sem=recv.at[k], device_id={'dp': at.opp}, device_id_type=MESH)

    ab, gg = pl.ds(0, 2), pl.ds(2, 1)

    def a1(k):
        return core_copy(ab, AB[k], k, a1_s, a1_r)

    def a2(k):
        return chip_copy(ab, AB[k], k, a2_s, a2_r)

    def g1(k):
        return core_copy(gg, GG[k], k, g1_s, g1_r)

    def g2(k):
        return chip_copy(gg, GG[k], k, g2_s, g2_r)

    def ab_partials(k):
        for load in gate_up_loads(k):
            load.wait()
        if k == 0:
            token_wait(0)

        def body(col, width):
            cs = pl.ds(col, width)
            part[0, :, cs] = dot_nn(cols[0], wg[:, cs])
            part[1, :, cs] = dot_nn(cols[0], wu[:, cs])

        column_tiles(AB[k], body, 512)
        a1(k).start()

    def ab_sum(k):
        a1(k).wait_recv()

        def add(col, width):
            cs = pl.ds(col, width)
            for i in range(2):
                part[i, opp, cs] += from_sib[i, theirs, cs]

        column_tiles(AB[k], add)
        a2(k).start()

    def g_partials(k):
        down_load(k).wait()
        if k == 0:
            token_wait(1)

        def body(col, width):
            cs = pl.ds(col, width)
            part[2, :, cs] = dot_nt(cols[1], wd[cs, :])

        column_tiles(GG[k], body, 512)
        g1(k).start()

    def g_sum(k):
        g1(k).wait_recv()

        def add(col, width):
            cs = pl.ds(col, width)
            part[2, opp, cs] += from_sib[2, theirs, cs]
            part[2, own, cs] += from_sib[2, mine, cs]

        column_tiles(GG[k], add)

    hg = Gather(at, act, pl.ds(0, 1), AB, [h_sems.at[i] for i in range(6)])
    qg = Gather(at, act, pl.ds(1, 2), GG, [q_sems.at[i] for i in range(6)])

    def hidden(k):
        a2(k).wait_recv()

        def body(col, width):
            cs = pl.ds(col, width)
            a, b = [part[i, own, cs] + from_sib[i, mine, cs] + from_opp[i, :, cs] for i in range(2)]
            part[0, own, cs] = a
            part[1, own, cs] = b
            act[0, own, cs] = (a * jax.nn.sigmoid(a) * b).astype(BF16)

        column_tiles(AB[k], body)
        hg.send(k)

    def act_t_store(k):
        cs = cols_of(AB[k])
        return pltpu.make_async_copy(act_t.at[cs, :], act_t_out.at[cs, :], t_sem.at[k])

    ysum = RowSum(at, y_acc, cols.at[0], y_got, y_ready, y_rows, (sum_s, sum_r, row_s, row_r))

    def outputs(k):
        hg.arrived(k)
        cs = cols_of(AB[k])

        def flip(col, width):
            ts = pl.ds(col, width)
            act_t[ts, :] = act[0, :, ts].T

        column_tiles(AB[k], flip)
        act_t_store(k).start()

        def tile(ns):
            y = dot_nn(act[0, :, cs], wd[cs, ns])
            y_acc[:, ns] = y if k == 0 else y_acc[:, ns] + y

        if k < NA - 1:
            @pl.loop(0, 1024 // MW)
            def _(n):
                tile(pl.ds(aligned(n * MW, 128), MW))
        else:
            for n in range(NT):
                tile(pl.ds(n * TW, TW))
                ysum.swap(n).start()

    def hidden_grads(k):
        g2(k).wait_recv()

        def body(col, width):
            cs = pl.ds(col, width)
            gate_grads(act, 1, own, cs, part[0, own, cs], part[1, own, cs], part[2, own, cs] + from_opp[2, :, cs])

        column_tiles(GG[k], body)
        qg.send(k)

    def act_store(k):
        cs = cols_of(GG[k])
        return pltpu.make_async_copy(act.at[pl.ds(1, 2), :, cs], act_out.at[:, :, cs], q_sem.at[k])

    def dx_part(k):
        qg.arrived(k)
        act_store(k).start()
        add_dx(dx_acc, act, 1, wg, wu, cols_of(GG[k]), k == 0)

    def dx_stores():
        for dt in range(2):
            for dd in range(4):
                row = 32 * (2 * (dd % 2) + dd // 2)
                yield pltpu.make_async_copy(dx_acc.at[pl.ds(row, 32), :], dx_out.at[4 * dt + dd],
                                            dx_sem.at[4 * dt + dd])

    stores = [
        pltpu.make_async_copy(cols.at[1], dy_cols_out, o_sem.at[0]),
        pltpu.make_async_copy(cols_t, cols_t_out, o_sem.at[1]),
        pltpu.make_async_copy(y_rows, y_out, o_sem.at[2]),
    ]

    for k in range(NA):
        ab_partials(k)
        if k >= 1:
            ab_sum(k - 1)
    ab_sum(NA - 1)
    for k in range(NG):
        g_partials(k)
        if k >= 1:
            g_sum(k - 1)
    g_sum(NG - 1)
    stores[0].start()
    for n in range(4):
        cols_t[n * 256:(n + 1) * 256, :] = cols[0, :, n * 256:(n + 1) * 256].T
    stores[1].start()
    for k in range(NA):
        hidden(k)
    for k in range(NG):
        g2(k).start()
    for k in range(NA):
        hg.forward(k)
        if k >= 1:
            outputs(k - 1)
    outputs(NA - 1)
    for k in range(NG):
        hidden_grads(k)
        if k == 2:
            for n in range(NT):
                ysum.finish(n)
    for k in range(NG):
        qg.forward(k)
        if k >= 1:
            dx_part(k - 1)
        if k == 1:
            ysum.collect()
            stores[2].start()
    dx_part(NG - 1)
    for store in dx_stores():
        store.start()
    for i in range(2):
        for q in range(3):
            token_copy(i, q, at.own_row).wait_send()
    for k in range(NA):
        a1(k).wait_send()
        a2(k).wait_send()
        act_t_store(k).wait()
    for k in range(NG):
        g1(k).wait_send()
        g2(k).wait_send()
        act_store(k).wait()
    hg.drain()
    qg.drain()
    ysum.drain()
    for store in stores:
        store.wait()
    for store in dx_stores():
        store.wait()


DMA = pltpu.SemaphoreType.DMA
ANY = pl.BlockSpec(memory_space=pl.ANY)
VMEM = pl.BlockSpec(memory_space=pltpu.VMEM)


def shape(dims, dtype):
    return jax.ShapeDtypeStruct(dims, dtype)


def front(x_rows, dy_rows, gate, up, down):
    return pl.pallas_call(
        front_kernel,
        name='front',
        out_shape=(shape((2, 128, HID), BF16), shape((HID, 128), BF16), shape((1024, 128), BF16),
                   shape((128, 1024), BF16), shape((32, 4096), BF16), shape((8, 32, 1024), F32)),
        in_specs=[ANY] * 5,
        out_specs=(ANY,) * 6,
        scratch_shapes=[
            pltpu.VMEM((32, 4096), BF16), pltpu.VMEM((32, 4096), BF16),
            pltpu.VMEM((1024, HID), BF16), pltpu.VMEM((1024, HID), BF16), pltpu.VMEM((HID, 1024), BF16),
            pltpu.VMEM((3, 128, HID), F32), pltpu.VMEM((3, 64, HID), F32), pltpu.VMEM((3, 32, HID), F32),
            pltpu.VMEM((3, 128, HID), BF16), pltpu.VMEM((HID, 128), BF16), pltpu.VMEM((2, 128, 1024), BF16),
            pltpu.VMEM((1024, 128), BF16), pltpu.VMEM((128, 1024), F32), pltpu.VMEM((128, 1024), F32),
            pltpu.VMEM((64, 1024), F32), pltpu.VMEM((64, 1024), BF16), pltpu.VMEM((32, 4096), BF16),
            DMA((2,)), DMA((2, NA)), DMA((NG,)), DMA((2, 3)), DMA((2, 3)),
            DMA((NA,)), DMA((NA,)), DMA((NA,)), DMA((NA,)),
            DMA((NG,)), DMA((NG,)), DMA((NG,)), DMA((NG,)),
            DMA((6, NA)), DMA((6, NG)), DMA((NT,)), DMA((NT,)), DMA((NT, 4)), DMA((NT, 4)),
            DMA((NA,)), DMA((NG,)), DMA((3,)), DMA((8,)),
        ],
        compiler_params=pltpu.CompilerParams(collective_id=0, has_side_effects=True, vmem_limit_bytes=VMEM_CAP),
        cost_estimate=pl.CostEstimate(flops=9 * 10**9, bytes_accessed=4 * 10**7, transcendentals=0),
    )(x_rows, dy_rows, gate, up, down)


TILE = 512
SLOTS = 6


def stream_tiles(compute, store, width):
    full, last = width // TILE, width % TILE

    def step(i, carry):
        slot = lax.rem(i, SLOTS)

        @pl.when(i >= SLOTS)
        def _():
            store(i - SLOTS, slot, TILE).wait()

        compute(i, slot, TILE)
        store(i, slot, TILE).start()
        return carry

    lax.fori_loop(0, full, step, 0)
    total = full
    if last:
        if full >= SLOTS:
            store(full - SLOTS, full % SLOTS, TILE).wait()
        compute(full, full % SLOTS, last)
        store(full, full % SLOTS, last).start()
        total += 1

    def drain():
        for i in range(max(0, total - SLOTS), total):
            store(i, i % SLOTS, TILE if i < full else last).wait()

    return drain


def column_job(left, right, ring, out, base, sem):
    def compute(i, slot, width):
        cs = pl.ds(aligned(i * TILE, 128), width)
        ring[slot, :, pl.ds(0, width)] = dot_nn(left[...], right[:, cs])

    def store(i, slot, width):
        return pltpu.make_async_copy(ring.at[slot, :, pl.ds(0, width)],
                                     out.at[:, pl.ds(aligned(base + i * TILE, 128), width)], sem.at[slot])

    return compute, store


def row_job(left, right, ring, out, sem):
    def compute(i, slot, width):
        ring[slot, pl.ds(0, width), :] = dot_nn(left[pl.ds(aligned(i * TILE, 128), width), :], right[...])

    def store(i, slot, width):
        return pltpu.make_async_copy(ring.at[slot, pl.ds(0, width), :],
                                     out.at[pl.ds(aligned(i * TILE, 128), width), :], sem.at[slot])

    return compute, store


def grads_first_kernel(act_t_hbm, dy_cols_hbm, cols_t_hbm, act_hbm, down_out, gate_out,
                       act_t, dy_cols, cols_t, act, ring_d, ring_c, in_sem, sem_d, sem_c):
    loads = [pltpu.make_async_copy(src, dst, in_sem.at[n]) for n, (src, dst) in enumerate((
        (dy_cols_hbm, dy_cols), (act_t_hbm, act_t), (cols_t_hbm, cols_t), (act_hbm.at[0], act)))]
    for load in loads:
        load.start()
    loads[0].wait()
    loads[1].wait()
    drain_d = stream_tiles(*row_job(act_t, dy_cols, ring_d, down_out, sem_d), HID)
    loads[2].wait()
    loads[3].wait()
    drain_c = stream_tiles(*column_job(cols_t, act, ring_c, gate_out, 0, sem_c), HID)
    drain_d()
    drain_c()


def grads_first(act_t, dy_cols, cols_t, act):
    return pl.pallas_call(
        grads_first_kernel,
        name='grads_first',
        out_shape=(shape((HID, 1024), F32), shape((1024, HID), F32)),
        in_specs=[ANY] * 4,
        out_specs=(ANY,) * 2,
        scratch_shapes=[pltpu.VMEM((HID, 128), BF16), pltpu.VMEM((128, 1024), BF16), pltpu.VMEM((1024, 128), BF16),
                        pltpu.VMEM((128, HID), BF16),
                        pltpu.VMEM((SLOTS, TILE, 1024), F32), pltpu.VMEM((SLOTS, 1024, TILE), F32),
                        DMA((4,)), DMA((SLOTS,)), DMA((SLOTS,))],
        compiler_params=pltpu.CompilerParams(vmem_limit_bytes=VMEM_CAP),
        cost_estimate=pl.CostEstimate(flops=2 * 10**10, bytes_accessed=5 * 10**7, transcendentals=0),
    )(act_t, dy_cols, cols_t, act)


def grads_last_kernel(cols_t_hbm, act_hbm, y_hbm, dy_hbm, got_hbm, up_out, y_out, dx_out,
                      cols_t, act, y_rows, dy_rows, got, dx_rows, ring, in_sem, sem, row_sem):
    loads = [pltpu.make_async_copy(src, dst, in_sem.at[n]) for n, (src, dst) in enumerate((
        (cols_t_hbm, cols_t), (act_hbm.at[1], act), (y_hbm, y_rows), (dy_hbm, dy_rows), (got_hbm, got)))]
    for load in loads:
        load.start()
    loads[0].wait()
    loads[1].wait()
    drain = stream_tiles(*column_job(cols_t, act, ring, up_out, 0, sem), HID)
    for load in loads[2:]:
        load.wait()
    copies = (pltpu.make_async_copy(y_rows, y_out, row_sem.at[0]), pltpu.make_async_copy(dx_rows, dx_out, row_sem.at[1]))
    copies[0].start()
    for d in range(4):
        cs = pl.ds(1024 * d, 1024)
        dx_rows[:, cs] = (dy_rows[:, cs].astype(F32) + (got[d] + got[4 + d])).astype(BF16)
    copies[1].start()
    drain()
    for copy in copies:
        copy.wait()


def grads_last(cols_t, act, y, dy, got):
    return pl.pallas_call(
        grads_last_kernel,
        name='grads_last',
        out_shape=(shape((1024, HID), F32), shape((32, 4096), BF16), shape((32, 4096), BF16)),
        in_specs=[ANY] * 5,
        out_specs=(ANY,) * 3,
        scratch_shapes=[pltpu.VMEM((1024, 128), BF16), pltpu.VMEM((128, HID), BF16), pltpu.VMEM((32, 4096), BF16),
                        pltpu.VMEM((32, 4096), BF16), pltpu.VMEM((8, 32, 1024), F32), pltpu.VMEM((32, 4096), BF16),
                        pltpu.VMEM((SLOTS, 1024, TILE), F32), DMA((5,)), DMA((SLOTS,)), DMA((2,))],
        compiler_params=pltpu.CompilerParams(vmem_limit_bytes=VMEM_CAP),
        cost_estimate=pl.CostEstimate(flops=10**10, bytes_accessed=3 * 10**7, transcendentals=0),
    )(cols_t, act, y, dy, got)


def solution(mesh):
    def device_pass(x_rows, gate_blk, up_blk, down_blk, dy_rows):
        act, act_t, cols_t, dy_cols, y_part, dx_part = front(x_rows, dy_rows, gate_blk, up_blk, down_blk)
        got = lax.all_to_all(dx_part, ('tp', 'dp'), 0, 0, tiled=True)
        dw_down, dw_gate = grads_first(act_t, dy_cols, cols_t, act)
        dw_up, y_rows, dx_rows = grads_last(cols_t, act, y_part, dy_rows, got)
        return y_rows, dx_rows, dw_gate, dw_up, dw_down

    row_spec = P('dp', None)
    weight_spec = P('dp', 'tp')
    down_spec = P('tp', 'dp')
    return jax.shard_map(device_pass, mesh=mesh,
                         in_specs=(row_spec, weight_spec, weight_spec, down_spec, row_spec),
                         out_specs=(row_spec, row_spec, weight_spec, weight_spec, down_spec),
                         check_vma=False)
```

time: 301 us -> 120 us (0.40)
  waiting for transfers between devices: 128 us -> 0.01 us
  Pallas kernels: 0 us -> 116 us
  matrix products: 77.6 us -> 0 us
  local copies, waits for them, and re-layouts: 47.9 us -> 0 us
  blocking collectives: 18.8 us -> 0 us
  between operations: 14.2 us -> 0.66 us
  other arithmetic: 6.39 us -> 0 us
  starting transfers between devices: 7.27 us -> 2.99 us
    pallas_call x0 -> x3, Pallas kernels: none -> 116 us  [the longest x1 90.1 us: front(): pl.pallas_call(front_kernel, name='front', out_shape=(shape((2, 128, HID)...]
    dot_general x9 -> x0, matrix products: 77.6 us -> none  [the longest x1 9.73 us: device_pass(): jnp.einsum('td,tf->df', x_cols, up_all, preferred_element_type=jnp.float32)]
    reduce_scatter x3 -> x0, waiting for transfers between devices: 72.7 us -> none  [the longest x1 33.1 us: device_pass(): lax.psum_scatter(gate_part, 'dp', scatter_dimension=0, tiled=True)]
    unnamed x10 -> x0, local copies, waits for them, and re-layouts: 45.5 us -> none
    all_gather x3 -> x0, waiting for transfers between devices: 34.5 us -> none  [the longest x1 14.5 us: device_pass(): hidden_all = lax.all_gather(hidden, 'dp', axis=0, tiled=True)]
    all_to_all x2 -> x0, blocking collectives: 18.8 us -> none  [the longest x1 10.4 us: device_pass(): dy_cols = lax.all_to_all(dy_rows, 'dp', 1, 0, tiled=True)]
    psum x1 -> x0, waiting for transfers between devices: 15.5 us -> none  [device_pass(): lax.psum(out_part, 'tp')]
    convert_element_type x3 -> x0, other arithmetic: 6.39 us -> none  [the longest x1 2.79 us: device_pass(): d_up = (grad_h * silu_gate).astype(jnp.bfloat16)]
  transfers between devices with their start and end apart: 9 -> 1, of which waited for: 8 -> 0; matrix products, arithmetic and copies ran while one was open for 36% -> 0% of each run, Pallas kernels for 0% -> 14%
where the time goes in v3:
time: 120 us
  Pallas kernels  116 us (97%)
  starting transfers between devices  2.99 us (2%)
    pallas_call x1, Pallas kernels, front(): pl.pallas_call(front_kernel, name='front', out_shape=(shape((2, 128, HID)...  90.1 us
    pallas_call x1, Pallas kernels, grads_first(): pl.pallas_call(grads_first_kernel, name='grads_first', out_shape=(shape((...  16.3 us
    pallas_call x1, Pallas kernels, grads_last(): pl.pallas_call(grads_last_kernel, name='grads_last', out_shape=(shape((10...  9.66 us
    all_to_all x1, starting transfers between devices, device_pass(): got = lax.all_to_all(dx_part, ('tp', 'dp'), 0, 0, tiled=True)  2.99 us
  transfers between devices with their start and end apart: 1, of which 0 were waited for; matrix products, arithmetic and copies ran while one was open for 0% of the time, Pallas kernels for 14%

profile of v3, /device:TPU:0, one launch (start us, length us, event | category | flops | bytes accessed | tf_op | source)
XLA Modules:
  0.0 119.7 jit_solution(16557408230052714554)
XLA Ops:
  0.6 90.1 %front.1 = (bf16[2,128,5504]{2,1,0:T(8,128)(2,1)}, bf16[5504,128]{1,0:T(8,128)(2,1)}, bf16[1024,128]{1,0:T(8,128)(2,1)}, bf16[128,1024]{1,0:T(8,128)(2,1)}, bf16...) custom-call(bf16[32,4096]{1,0:T(8,128)(2,1)} %x_hbm.1, bf16[32,4096]{1,0:T(8,128)(2,1)} %dy_hbm.3, ...), custom_call_target="tpu_custom_call" | custom-call | flops 8999999488 | bytes 40000000 | tf_op jit(solution)/shard_map/front/pallas_call | solution.py:483
  90.7 3.0 %all-to-all-start = ((f32[8,32,1024]{2,1,0:T(8,128)}), f32[8,32,1024]{2,1,0:T(8,128)}, u32[]{:S(2)}, u32[]{:S(2)}) async-start(f32[8,32,1024]{2,1,0:T(8,128)} %get-tuple-element.19), calls=%async_computation | async-start | bytes 2097152 | tf_op jit(solution)/shard_map/all_to_all | solution.py:637
  93.7 16.3 %grads_first.1 = (f32[5504,1024]{1,0:T(8,128)}, f32[1024,5504]{1,0:T(8,128)}) custom-call(bf16[5504,128]{1,0:T(8,128)(2,1)} %get-tuple-element.22.act_t_hbm, bf16[128,1024]{1,0:T(8,128)(2,1)} %get-tuple-element.23.dy_cols_hbm, bf16[1024,128]{1,0:T(8,128)(2,1)} %get-tuple-element.16.cols_t_hbm, bf16[2,128,5504]{2,1,0:T(8,128)(2,1)} %get-tuple-element.17.act_hbm), custom_call_target="tpu_custom_call" | custom-call | flops 20000000000 | bytes 50000000 | tf_op jit(solution)/shard_map/grads_first/pallas_call | solution.py:582
  110.1 0.0 all-to-all-done.got_hbm
  110.1 9.7 %grads_last.1 = (f32[1024,5504]{1,0:T(8,128)}, bf16[32,4096]{1,0:T(8,128)(2,1)}, bf16[32,4096]{1,0:T(8,128)(2,1)}) custom-call(bf16[1024,128]{1,0:T(8,128)(2,1)} %get-tuple-element.16.cols_t_hbm, bf16[2,128,5504]{2,1,0:T(8,128)(2,1)} %get-tuple-element.17.act_hbm, bf16[32,4096]{1,0:T(8,128)(2,1)} %get-tuple-element.18.y_hbm, bf16[32,4096]{1,0:T(8,128)(2,1)} %dy_hbm.3, ...), custom_call_target="tpu_custom_call" | custom-call | flops 10000000000 | bytes 30000000 | tf_op jit(solution)/shard_map/grads_last/pallas_call | solution.py:620
Async XLA Ops:
  90.7 19.4 %all-to-all-start = ((f32[8,32,1024]{2,1,0:T(8,128)}), f32[8,32,1024]{2,1,0:T(8,128)}, u32[]{:S(2)}, u32[]{:S(2)}) async-start(f32[8,32,1024]{2,1,0:T(8,128)} %get-tuple-element.19), calls=%async_computation | async-start | bytes 2097152 | tf_op jit(solution)/shard_map/all_to_all | solution.py:637

commit v4 on v3

--- a/solution.py
+++ b/solution.py
@@ -19,8 +19,8 @@
     return tuple(out)
 
 
-AB = chunks(0, (512, 512, 1024, 1024, 1024, 1024, 384))
-GG = chunks(0, (1024, 1024, 1024, 1024, 768, 384, 256))
+AB = chunks(0, (256, 256, 512, 1024, 1024, 1024, 1024, 384))
+GG = chunks(0, (1024, 1024, 1024, 1024, 768, 512, 128))
 NA, NG = len(AB), len(GG)
 NT = 4
 TW = 1024 // NT
@@ -149,6 +149,12 @@
             send_sem=self.row_s.at[n, 2 * ox + ot], recv_sem=self.row_r.at[n, at.d],
             device_id={'tp': 1 - at.t if ot else at.t, 'dp': 2 * chip + at.t}, device_id_type=MESH)
 
+    def own_copy(self, n):
+        at = self.at
+        return pltpu.make_async_copy(
+            self.ready.at[pl.ds(aligned(32 * at.cx, 32), 32), self.tile(n)],
+            self.landed.at[:, pl.ds(aligned(1024 * at.d + n * TW, 128), TW)], self.row_r.at[n, at.d])
+
     def row_arrive(self, n, s):
         return pltpu.make_async_remote_copy(
             src_ref=self.ready.at[pl.ds(0, 32), self.tile(n)],
@@ -170,8 +176,7 @@
 
         @pl.when(self.local)
         def _():
-            self.landed[:, pl.ds(aligned(1024 * at.d + n * TW, 128), TW)] = (
-                self.ready[pl.ds(aligned(32 * at.cx, 32), 32), ns])
+            self.own_copy(n).start()
 
     def collect(self):
         for n in range(NT):
@@ -180,6 +185,10 @@
                 def _():
                     self.row_arrive(n, s).wait_recv()
 
+            @pl.when(self.local)
+            def _():
+                self.own_copy(n).wait()
+
     def drain(self):
         for n in range(NT):
             self.swap(n).wait_send()
@@ -208,7 +217,7 @@
 
 def front_kernel(x_hbm, dy_hbm, wg_hbm, wu_hbm, wd_hbm,
                  act_out, act_t_out, cols_t_out, dy_cols_out, y_out, dx_out,
-                 x_ref, dy_ref, wg, wu, wd, part, from_sib, from_opp, act, act_t, cols, cols_t, y_acc, dx_acc, y_got, y_ready, y_rows,
+                 x_ref, dy_ref, wg, wu, wd, part, from_sib, from_opp, act, act_t, cols, cols_t, y_acc, dx_acc, y_got, y_ready,
                  in_sem, gu_sem, d_sem, x_send, x_recv, a1_s, a1_r, a2_s, a2_r, g1_s, g1_r, g2_s, g2_r,
                  h_sems, q_sems, sum_s, sum_r, row_s, row_r, t_sem, q_sem, o_sem, dx_sem):
     at = Place()
@@ -354,7 +363,7 @@
         cs = cols_of(AB[k])
         return pltpu.make_async_copy(act_t.at[cs, :], act_t_out.at[cs, :], t_sem.at[k])
 
-    ysum = RowSum(at, y_acc, cols.at[0], y_got, y_ready, y_rows, (sum_s, sum_r, row_s, row_r))
+    ysum = RowSum(at, y_acc, cols.at[0], y_got, y_ready, y_out, (sum_s, sum_r, row_s, row_r))
 
     def outputs(k):
         hg.arrived(k)
@@ -409,7 +418,6 @@
     stores = [
         pltpu.make_async_copy(cols.at[1], dy_cols_out, o_sem.at[0]),
         pltpu.make_async_copy(cols_t, cols_t_out, o_sem.at[1]),
-        pltpu.make_async_copy(y_rows, y_out, o_sem.at[2]),
     ]
 
     for k in range(NA):
@@ -437,19 +445,16 @@
     outputs(NA - 1)
     for k in range(NG):
         hidden_grads(k)
-        if k == 2:
-            for n in range(NT):
-                ysum.finish(n)
+    for n in range(NT):
+        ysum.finish(n)
     for k in range(NG):
         qg.forward(k)
         if k >= 1:
             dx_part(k - 1)
-        if k == 1:
-            ysum.collect()
-            stores[2].start()
     dx_part(NG - 1)
     for store in dx_stores():
         store.start()
+    ysum.collect()
     for i in range(2):
         for q in range(3):
             token_copy(i, q, at.own_row).wait_send()
@@ -493,12 +498,12 @@
             pltpu.VMEM((3, 128, HID), F32), pltpu.VMEM((3, 64, HID), F32), pltpu.VMEM((3, 32, HID), F32),
             pltpu.VMEM((3, 128, HID), BF16), pltpu.VMEM((HID, 128), BF16), pltpu.VMEM((2, 128, 1024), BF16),
             pltpu.VMEM((1024, 128), BF16), pltpu.VMEM((128, 1024), F32), pltpu.VMEM((128, 1024), F32),
-            pltpu.VMEM((64, 1024), F32), pltpu.VMEM((64, 1024), BF16), pltpu.VMEM((32, 4096), BF16),
+            pltpu.VMEM((64, 1024), F32), pltpu.VMEM((64, 1024), BF16),
             DMA((2,)), DMA((2, NA)), DMA((NG,)), DMA((2, 3)), DMA((2, 3)),
             DMA((NA,)), DMA((NA,)), DMA((NA,)), DMA((NA,)),
             DMA((NG,)), DMA((NG,)), DMA((NG,)), DMA((NG,)),
             DMA((6, NA)), DMA((6, NG)), DMA((NT,)), DMA((NT,)), DMA((NT, 4)), DMA((NT, 4)),
-            DMA((NA,)), DMA((NG,)), DMA((3,)), DMA((8,)),
+            DMA((NA,)), DMA((NG,)), DMA((2,)), DMA((8,)),
         ],
         compiler_params=pltpu.CompilerParams(collective_id=0, has_side_effects=True, vmem_limit_bytes=VMEM_CAP),
         cost_estimate=pl.CostEstimate(flops=9 * 10**9, bytes_accessed=4 * 10**7, transcendentals=0),
@@ -509,8 +514,11 @@
 SLOTS = 6
 
 
-def stream_tiles(compute, store, width):
+def stream_tiles(compute, store, width, rest):
     full, last = width // TILE, width % TILE
+    compute(0, 0, TILE)
+    store(0, 0, TILE).start()
+    rest()
 
     def step(i, carry):
         slot = lax.rem(i, SLOTS)
@@ -523,7 +531,7 @@
         store(i, slot, TILE).start()
         return carry
 
-    lax.fori_loop(0, full, step, 0)
+    lax.fori_loop(1, full, step, 0)
     total = full
     if last:
         if full >= SLOTS:
@@ -539,6 +547,18 @@
     return drain
 
 
+def load_all(pairs, sem):
+    loads = [pltpu.make_async_copy(src, dst, sem.at[n]) for n, (src, dst) in enumerate(pairs)]
+    for load in loads:
+        load.start()
+
+    def wait(*which):
+        for n in which:
+            loads[n].wait()
+
+    return wait
+
+
 def column_job(left, right, ring, out, base, sem):
     def compute(i, slot, width):
         cs = pl.ds(aligned(i * TILE, 128), width)
@@ -564,16 +584,12 @@
 
 def grads_first_kernel(act_t_hbm, dy_cols_hbm, cols_t_hbm, act_hbm, down_out, gate_out,
                        act_t, dy_cols, cols_t, act, ring_d, ring_c, in_sem, sem_d, sem_c):
-    loads = [pltpu.make_async_copy(src, dst, in_sem.at[n]) for n, (src, dst) in enumerate((
-        (dy_cols_hbm, dy_cols), (act_t_hbm, act_t), (cols_t_hbm, cols_t), (act_hbm.at[0], act)))]
-    for load in loads:
-        load.start()
-    loads[0].wait()
-    loads[1].wait()
-    drain_d = stream_tiles(*row_job(act_t, dy_cols, ring_d, down_out, sem_d), HID)
-    loads[2].wait()
-    loads[3].wait()
-    drain_c = stream_tiles(*column_job(cols_t, act, ring_c, gate_out, 0, sem_c), HID)
+    head, tail = pl.ds(0, TILE), pl.ds(TILE, HID - TILE)
+    wait = load_all(((dy_cols_hbm, dy_cols), (act_t_hbm.at[head, :], act_t.at[head, :]),
+                     (act_t_hbm.at[tail, :], act_t.at[tail, :]), (cols_t_hbm, cols_t), (act_hbm.at[0], act)), in_sem)
+    wait(0, 1)
+    drain_d = stream_tiles(*row_job(act_t, dy_cols, ring_d, down_out, sem_d), HID, lambda: wait(2, 3, 4))
+    drain_c = stream_tiles(*column_job(cols_t, act, ring_c, gate_out, 0, sem_c), HID, lambda: None)
     drain_d()
     drain_c()
 
@@ -588,7 +604,7 @@
         scratch_shapes=[pltpu.VMEM((HID, 128), BF16), pltpu.VMEM((128, 1024), BF16), pltpu.VMEM((1024, 128), BF16),
                         pltpu.VMEM((128, HID), BF16),
                         pltpu.VMEM((SLOTS, TILE, 1024), F32), pltpu.VMEM((SLOTS, 1024, TILE), F32),
-                        DMA((4,)), DMA((SLOTS,)), DMA((SLOTS,))],
+                        DMA((5,)), DMA((SLOTS,)), DMA((SLOTS,))],
         compiler_params=pltpu.CompilerParams(vmem_limit_bytes=VMEM_CAP),
         cost_estimate=pl.CostEstimate(flops=2 * 10**10, bytes_accessed=5 * 10**7, transcendentals=0),
     )(act_t, dy_cols, cols_t, act)
@@ -596,15 +612,13 @@
 
 def grads_last_kernel(cols_t_hbm, act_hbm, y_hbm, dy_hbm, got_hbm, up_out, y_out, dx_out,
                       cols_t, act, y_rows, dy_rows, got, dx_rows, ring, in_sem, sem, row_sem):
-    loads = [pltpu.make_async_copy(src, dst, in_sem.at[n]) for n, (src, dst) in enumerate((
-        (cols_t_hbm, cols_t), (act_hbm.at[1], act), (y_hbm, y_rows), (dy_hbm, dy_rows), (got_hbm, got)))]
-    for load in loads:
-        load.start()
-    loads[0].wait()
-    loads[1].wait()
-    drain = stream_tiles(*column_job(cols_t, act, ring, up_out, 0, sem), HID)
-    for load in loads[2:]:
-        load.wait()
+    head, tail = pl.ds(0, TILE), pl.ds(TILE, HID - TILE)
+    wait = load_all(((cols_t_hbm, cols_t), (act_hbm.at[1, :, head], act.at[:, head]),
+                     (act_hbm.at[1, :, tail], act.at[:, tail]), (y_hbm, y_rows), (dy_hbm, dy_rows),
+                     (got_hbm, got)), in_sem)
+    wait(0, 1)
+    drain = stream_tiles(*column_job(cols_t, act, ring, up_out, 0, sem), HID, lambda: wait(2))
+    wait(3, 4, 5)
     copies = (pltpu.make_async_copy(y_rows, y_out, row_sem.at[0]), pltpu.make_async_copy(dx_rows, dx_out, row_sem.at[1]))
     copies[0].start()
     for d in range(4):
@@ -625,7 +639,7 @@
         out_specs=(ANY,) * 3,
         scratch_shapes=[pltpu.VMEM((1024, 128), BF16), pltpu.VMEM((128, HID), BF16), pltpu.VMEM((32, 4096), BF16),
                         pltpu.VMEM((32, 4096), BF16), pltpu.VMEM((8, 32, 1024), F32), pltpu.VMEM((32, 4096), BF16),
-                        pltpu.VMEM((SLOTS, 1024, TILE), F32), DMA((5,)), DMA((SLOTS,)), DMA((2,))],
+                        pltpu.VMEM((SLOTS, 1024, TILE), F32), DMA((6,)), DMA((SLOTS,)), DMA((2,))],
         compiler_params=pltpu.CompilerParams(vmem_limit_bytes=VMEM_CAP),
         cost_estimate=pl.CostEstimate(flops=10**10, bytes_accessed=3 * 10**7, transcendentals=0),
     )(cols_t, act, y, dy, got)

time: 120 us -> 116 us (0.967)
  Pallas kernels: 116 us -> 112 us
    pallas_call x1, Pallas kernels: 90.1 us -> 86.8 us  [front(): pl.pallas_call(front_kernel, name='front', out_shape=(shape((2, 128, HID)...]
where the time goes in v4:
time: 116 us
  Pallas kernels  112 us (97%)
  starting transfers between devices  2.99 us (3%)
    pallas_call x1, Pallas kernels, front(): pl.pallas_call(front_kernel, name='front', out_shape=(shape((2, 128, HID)...  86.8 us
    pallas_call x1, Pallas kernels, grads_first(): pl.pallas_call(grads_first_kernel, name='grads_first', out_shape=(shape((...  16.2 us
    pallas_call x1, Pallas kernels, grads_last(): pl.pallas_call(grads_last_kernel, name='grads_last', out_shape=(shape((10...  9.21 us
    all_to_all x1, starting transfers between devices, device_pass(): got = lax.all_to_all(dx_part, ('tp', 'dp'), 0, 0, tiled=True)  2.99 us
  transfers between devices with their start and end apart: 1, of which 0 were waited for; matrix products, arithmetic and copies ran while one was open for 0% of the time, Pallas kernels for 14%

profile of v4, /device:TPU:0, one launch (start us, length us, event | category | flops | bytes accessed | tf_op | source)
XLA Modules:
  0.0 115.8 jit_solution(16074209652737471132)
XLA Ops:
  0.6 86.8 %front.1 = (bf16[2,128,5504]{2,1,0:T(8,128)(2,1)}, bf16[5504,128]{1,0:T(8,128)(2,1)}, bf16[1024,128]{1,0:T(8,128)(2,1)}, bf16[128,1024]{1,0:T(8,128)(2,1)}, bf16...) custom-call(bf16[32,4096]{1,0:T(8,128)(2,1)} %x_hbm.1, bf16[32,4096]{1,0:T(8,128)(2,1)} %dy_hbm.3, ...), custom_call_target="tpu_custom_call" | custom-call | flops 8999999488 | bytes 40000000 | tf_op jit(solution)/shard_map/front/pallas_call | solution.py:488
  87.4 3.0 %all-to-all-start = ((f32[8,32,1024]{2,1,0:T(8,128)}), f32[8,32,1024]{2,1,0:T(8,128)}, u32[]{:S(2)}, u32[]{:S(2)}) async-start(f32[8,32,1024]{2,1,0:T(8,128)} %get-tuple-element.19), calls=%async_computation | async-start | bytes 2097152 | tf_op jit(solution)/shard_map/all_to_all | solution.py:651
  90.4 16.2 %grads_first.1 = (f32[5504,1024]{1,0:T(8,128)}, f32[1024,5504]{1,0:T(8,128)}) custom-call(bf16[5504,128]{1,0:T(8,128)(2,1)} %get-tuple-element.22.act_t_hbm, bf16[128,1024]{1,0:T(8,128)(2,1)} %get-tuple-element.23.dy_cols_hbm, bf16[1024,128]{1,0:T(8,128)(2,1)} %get-tuple-element.16.cols_t_hbm, bf16[2,128,5504]{2,1,0:T(8,128)(2,1)} %get-tuple-element.17.act_hbm), custom_call_target="tpu_custom_call" | custom-call | flops 20000000000 | bytes 50000000 | tf_op jit(solution)/shard_map/grads_first/pallas_call | solution.py:598
  106.6 0.0 all-to-all-done.got_hbm
  106.6 9.2 %grads_last.1 = (f32[1024,5504]{1,0:T(8,128)}, bf16[32,4096]{1,0:T(8,128)(2,1)}, bf16[32,4096]{1,0:T(8,128)(2,1)}) custom-call(bf16[1024,128]{1,0:T(8,128)(2,1)} %get-tuple-element.16.cols_t_hbm, bf16[2,128,5504]{2,1,0:T(8,128)(2,1)} %get-tuple-element.17.act_hbm, bf16[32,4096]{1,0:T(8,128)(2,1)} %get-tuple-element.18.y_hbm, bf16[32,4096]{1,0:T(8,128)(2,1)} %dy_hbm.3, ...), custom_call_target="tpu_custom_call" | custom-call | flops 10000000000 | bytes 30000000 | tf_op jit(solution)/shard_map/grads_last/pallas_call | solution.py:634
Async XLA Ops:
  87.4 19.2 %all-to-all-start = ((f32[8,32,1024]{2,1,0:T(8,128)}), f32[8,32,1024]{2,1,0:T(8,128)}, u32[]{:S(2)}, u32[]{:S(2)}) async-start(f32[8,32,1024]{2,1,0:T(8,128)} %get-tuple-element.19), calls=%async_computation | async-start | bytes 2097152 | tf_op jit(solution)/shard_map/all_to_all | solution.py:651

commit v5 on v4

--- a/solution.py
+++ b/solution.py
@@ -19,8 +19,8 @@
     return tuple(out)
 
 
-AB = chunks(0, (256, 256, 512, 1024, 1024, 1024, 1024, 384))
-GG = chunks(0, (1024, 1024, 1024, 1024, 768, 512, 128))
+AB = chunks(0, (512, 512, 1024, 1024, 1024, 1024, 384))
+GG = chunks(0, (512, 1024, 1024, 1024, 1024, 512, 256, 128))
 NA, NG = len(AB), len(GG)
 NT = 4
 TW = 1024 // NT
@@ -72,6 +72,11 @@
         self.keep = pl.ds(aligned(64 * self.t, 64), 64)
         self.give = pl.ds(aligned(64 * (1 - self.t), 64), 64)
 
+    def rows(self, k):
+        if k == 0:
+            return self.opp_row, self.own_row, self.far_row, self.sib_row
+        return self.own_row, self.opp_row, self.sib_row, self.far_row
+
     def enter(self):
         barrier = pltpu.get_barrier_semaphore()
         for dt in range(2):
@@ -95,28 +100,28 @@
             send_sem=send.at[k], recv_sem=recv.at[k], device_id={'dp': to}, device_id_type=MESH)
 
     def out_opp(self, k, dst=None):
-        at = self.at
-        return self.copy(k, at.own_row, at.own_row if dst is None else dst, self.opp_s, self.opp_r, at.opp)
+        own = self.at.rows(k)[0]
+        return self.copy(k, own, own if dst is None else dst, self.opp_s, self.opp_r, self.at.opp)
 
     def out_sib(self, k, dst=None):
-        at = self.at
-        return self.copy(k, at.own_row, at.own_row if dst is None else dst, self.sib_s, self.sib_r, at.sib)
+        own = self.at.rows(k)[0]
+        return self.copy(k, own, own if dst is None else dst, self.sib_s, self.sib_r, self.at.sib)
 
     def out_fwd(self, k, dst=None):
-        at = self.at
-        return self.copy(k, at.opp_row, at.opp_row if dst is None else dst, self.fwd_s, self.fwd_r, at.sib)
+        opp = self.at.rows(k)[1]
+        return self.copy(k, opp, opp if dst is None else dst, self.fwd_s, self.fwd_r, self.at.sib)
 
     def send(self, k):
         self.out_opp(k).start()
         self.out_sib(k).start()
 
     def forward(self, k):
-        self.out_opp(k, self.at.opp_row).wait_recv()
+        self.out_opp(k, self.at.rows(k)[1]).wait_recv()
         self.out_fwd(k).start()
 
     def arrived(self, k):
-        self.out_sib(k, self.at.sib_row).wait_recv()
-        self.out_fwd(k, self.at.far_row).wait_recv()
+        self.out_sib(k, self.at.rows(k)[2]).wait_recv()
+        self.out_fwd(k, self.at.rows(k)[3]).wait_recv()
 
     def drain(self):
         for k in range(len(self.chunks)):
@@ -167,7 +172,7 @@
         self.swap(n).wait_recv()
         total = self.acc[at.keep, ns] + self.got[:, ns]
         self.ready[:, ns] = (self.kept[at.keep, ns].astype(F32) + total).astype(BF16)
-        for ox, ot in ((1, 1), (1, 0), (0, 1)):
+        for ox, ot in ((1, 1), (0, 1)):
             self.row_copy(n, ox, ot).start()
 
         @pl.when(jnp.logical_not(self.local))
@@ -207,18 +212,10 @@
     act[slot + 1, own, cs] = (g * (a * s)).astype(BF16)
 
 
-def add_dx(acc, act, slot, wg, wu, cs, fresh):
-    @pl.loop(0, 1024 // MW)
-    def _(n):
-        ns = pl.ds(aligned(n * MW, 128), MW)
-        dx = dot_nt(act[slot, :, cs], wg[ns, cs]) + dot_nt(act[slot + 1, :, cs], wu[ns, cs])
-        acc[:, ns] = dx if fresh else acc[:, ns] + dx
-
-
 def front_kernel(x_hbm, dy_hbm, wg_hbm, wu_hbm, wd_hbm,
                  act_out, act_t_out, cols_t_out, dy_cols_out, y_out, dx_out,
                  x_ref, dy_ref, wg, wu, wd, part, from_sib, from_opp, act, act_t, cols, cols_t, y_acc, dx_acc, y_got, y_ready,
-                 in_sem, gu_sem, d_sem, x_send, x_recv, a1_s, a1_r, a2_s, a2_r, g1_s, g1_r, g2_s, g2_r,
+                 in_sem, gu_sem, d_sem, x_send, x_recv, a0_s, a0_r, a1_s, a1_r, a2_s, a2_r, g1_s, g1_r, g2_s, g2_r,
                  h_sems, q_sems, sum_s, sum_r, row_s, row_r, t_sem, q_sem, o_sem, dx_sem):
     at = Place()
     own, opp = pl.ds(at.own_row, 32), pl.ds(at.opp_row, 32)
@@ -266,9 +263,9 @@
     for i in range(2):
         cols[i, own, :] = tokens[i][:, pl.ds(aligned(1024 * at.d, 128), 1024)]
 
-    def token_wait(i):
-        for q, row in enumerate((at.sib_row, at.opp_row, at.far_row)):
-            token_copy(i, q, row).wait_recv()
+    def token_wait(i, which=(0, 1, 2)):
+        for q in which:
+            token_copy(i, q, (at.sib_row, at.opp_row, at.far_row)[q]).wait_recv()
 
     def core_copy(parts, chunk, k, send, recv):
         cs = cols_of(chunk)
@@ -279,7 +276,7 @@
     def chip_copy(parts, chunk, k, send, recv):
         cs = cols_of(chunk)
         return pltpu.make_async_remote_copy(
-            src_ref=part.at[parts, opp, cs], dst_ref=from_opp.at[parts, :, cs],
+            src_ref=part.at[parts, pl.ds(at.rows(k)[1], 32), cs], dst_ref=from_opp.at[parts, :, cs],
             send_sem=send.at[k], recv_sem=recv.at[k], device_id={'dp': at.opp}, device_id_type=MESH)
 
     ab, gg = pl.ds(0, 2), pl.ds(2, 1)
@@ -295,12 +292,40 @@
 
     def g2(k):
         return chip_copy(gg, GG[k], k, g2_s, g2_r)
+
+    def first_core_copy(which):
+        cs = cols_of(AB[0])
+        return pltpu.make_async_remote_copy(
+            src_ref=part.at[ab, pl.ds((at.sib_row, at.far_row)[which], 32), cs],
+            dst_ref=from_sib.at[ab, (mine, theirs)[which], cs],
+            send_sem=a0_s.at[which], recv_sem=a0_r.at[which], device_id={'dp': at.sib}, device_id_type=MESH)
+
+    def first_partials(which):
+        upper, lower = [pl.ds(row, 32) for row in ((at.own_row, at.sib_row), (at.opp_row, at.far_row))[which]]
+        cs = cols_of(AB[0])
+        rows = jnp.concatenate([cols[0, upper, :], cols[0, lower, :]], axis=0)
+        for i, w in enumerate((wg, wu)):
+            out = dot_nn(rows, w[:, cs])
+            part[i, upper, cs] = out[:32]
+            part[i, lower, cs] = out[32:]
+        first_core_copy(which).start()
+
+    def first_chunk():
+        for load in gate_up_loads(0):
+            load.wait()
+        token_wait(0, (0,))
+        first_partials(0)
+        first_core_copy(0).wait_recv()
+        cs = cols_of(AB[0])
+        for i in range(2):
+            part[i, own, cs] += from_sib[i, mine, cs]
+        a2(0).start()
+        token_wait(0, (1, 2))
+        first_partials(1)
 
     def ab_partials(k):
         for load in gate_up_loads(k):
             load.wait()
-        if k == 0:
-            token_wait(0)
 
         def body(col, width):
             cs = pl.ds(col, width)
@@ -347,14 +372,18 @@
     qg = Gather(at, act, pl.ds(1, 2), GG, [q_sems.at[i] for i in range(6)])
 
     def hidden(k):
+        if k == 0:
+            first_core_copy(1).wait_recv()
         a2(k).wait_recv()
+        here = pl.ds(at.rows(k)[0], 32)
+        core = theirs if k == 0 else mine
 
         def body(col, width):
             cs = pl.ds(col, width)
-            a, b = [part[i, own, cs] + from_sib[i, mine, cs] + from_opp[i, :, cs] for i in range(2)]
-            part[0, own, cs] = a
-            part[1, own, cs] = b
-            act[0, own, cs] = (a * jax.nn.sigmoid(a) * b).astype(BF16)
+            a, b = [part[i, here, cs] + from_sib[i, core, cs] + from_opp[i, :, cs] for i in range(2)]
+            part[0, here, cs] = a
+            part[1, here, cs] = b
+            act[0, here, cs] = (a * jax.nn.sigmoid(a) * b).astype(BF16)
 
         column_tiles(AB[k], body)
         hg.send(k)
@@ -391,10 +420,11 @@
 
     def hidden_grads(k):
         g2(k).wait_recv()
+        here = pl.ds(at.rows(k)[0], 32)
 
         def body(col, width):
             cs = pl.ds(col, width)
-            gate_grads(act, 1, own, cs, part[0, own, cs], part[1, own, cs], part[2, own, cs] + from_opp[2, :, cs])
+            gate_grads(act, 1, here, cs, part[0, here, cs], part[1, here, cs], part[2, here, cs] + from_opp[2, :, cs])
 
         column_tiles(GG[k], body)
         qg.send(k)
@@ -403,26 +433,31 @@
         cs = cols_of(GG[k])
         return pltpu.make_async_copy(act.at[pl.ds(1, 2), :, cs], act_out.at[:, :, cs], q_sem.at[k])
 
-    def dx_part(k):
-        qg.arrived(k)
-        act_store(k).start()
-        add_dx(dx_acc, act, 1, wg, wu, cols_of(GG[k]), k == 0)
-
-    def dx_stores():
+    def dx_part(k, n):
+        cs, ns = cols_of(GG[k]), pl.ds(n * MW, MW)
+        if n == 0:
+            qg.arrived(k)
+            act_store(k).start()
+        dx = dot_nt(act[1, :, cs], wg[ns, cs]) + dot_nt(act[2, :, cs], wu[ns, cs])
+        dx_acc[:, ns] = dx if k == 0 else dx_acc[:, ns] + dx
+
+    def dx_stores(n):
+        ns = pl.ds(n * MW, MW)
         for dt in range(2):
             for dd in range(4):
                 row = 32 * (2 * (dd % 2) + dd // 2)
-                yield pltpu.make_async_copy(dx_acc.at[pl.ds(row, 32), :], dx_out.at[4 * dt + dd],
-                                            dx_sem.at[4 * dt + dd])
+                yield pltpu.make_async_copy(dx_acc.at[pl.ds(row, 32), ns], dx_out.at[4 * dt + dd, :, ns],
+                                            dx_sem.at[n, 4 * dt + dd])
 
     stores = [
         pltpu.make_async_copy(cols.at[1], dy_cols_out, o_sem.at[0]),
         pltpu.make_async_copy(cols_t, cols_t_out, o_sem.at[1]),
     ]
 
-    for k in range(NA):
+    first_chunk()
+    for k in range(1, NA):
         ab_partials(k)
-        if k >= 1:
+        if k >= 2:
             ab_sum(k - 1)
     ab_sum(NA - 1)
     for k in range(NG):
@@ -447,19 +482,30 @@
         hidden_grads(k)
     for n in range(NT):
         ysum.finish(n)
-    for k in range(NG):
-        qg.forward(k)
-        if k >= 1:
-            dx_part(k - 1)
-    dx_part(NG - 1)
-    for store in dx_stores():
-        store.start()
+    for n in range(NT):
+        ysum.row_copy(n, 1, 0).start()
+    for step in ('f0', 'f1', 'd0', 'D0', 'f2', 'd1', 'D1', 'd2', 'f3', 'D2', 'f4', 'd3', 'f5', 'D3', 'f6', 'f7',
+                 'd4', 'D4', 'd5', 'D5', 'd6', 'D6', 'd7'):
+        k = int(step[1])
+        if step[0] == 'f':
+            qg.forward(k)
+        else:
+            dx_part(k, 0 if step[0] == 'd' else 1)
+    for n in range(2):
+        if n:
+            dx_part(NG - 1, n)
+        for store in dx_stores(n):
+            store.start()
     ysum.collect()
     for i in range(2):
         for q in range(3):
             token_copy(i, q, at.own_row).wait_send()
     for k in range(NA):
-        a1(k).wait_send()
+        if k == 0:
+            first_core_copy(0).wait_send()
+            first_core_copy(1).wait_send()
+        else:
+            a1(k).wait_send()
         a2(k).wait_send()
         act_t_store(k).wait()
     for k in range(NG):
@@ -471,8 +517,9 @@
     ysum.drain()
     for store in stores:
         store.wait()
-    for store in dx_stores():
-        store.wait()
+    for n in range(2):
+        for store in dx_stores(n):
+            store.wait()
 
 
 DMA = pltpu.SemaphoreType.DMA
@@ -500,10 +547,10 @@
             pltpu.VMEM((1024, 128), BF16), pltpu.VMEM((128, 1024), F32), pltpu.VMEM((128, 1024), F32),
             pltpu.VMEM((64, 1024), F32), pltpu.VMEM((64, 1024), BF16),
             DMA((2,)), DMA((2, NA)), DMA((NG,)), DMA((2, 3)), DMA((2, 3)),
-            DMA((NA,)), DMA((NA,)), DMA((NA,)), DMA((NA,)),
+            DMA((2,)), DMA((2,)), DMA((NA,)), DMA((NA,)), DMA((NA,)), DMA((NA,)),
             DMA((NG,)), DMA((NG,)), DMA((NG,)), DMA((NG,)),
             DMA((6, NA)), DMA((6, NG)), DMA((NT,)), DMA((NT,)), DMA((NT, 4)), DMA((NT, 4)),
-            DMA((NA,)), DMA((NG,)), DMA((2,)), DMA((8,)),
+            DMA((NA,)), DMA((NG,)), DMA((2,)), DMA((2, 8)),
         ],
         compiler_params=pltpu.CompilerParams(collective_id=0, has_side_effects=True, vmem_limit_bytes=VMEM_CAP),
         cost_estimate=pl.CostEstimate(flops=9 * 10**9, bytes_accessed=4 * 10**7, transcendentals=0),

time: 116 us -> 115 us (level)
  no operation moved by 1% of the time
where the time goes in v5:
time: 115 us
  Pallas kernels  111 us (97%)
  starting transfers between devices  3.17 us (3%)
    pallas_call x1, Pallas kernels, front(): pl.pallas_call(front_kernel, name='front', out_shape=(shape((2, 128, HID)...  85.8 us
    pallas_call x1, Pallas kernels, grads_first(): pl.pallas_call(grads_first_kernel, name='grads_first', out_shape=(shape((...  16.2 us
    pallas_call x1, Pallas kernels, grads_last(): pl.pallas_call(grads_last_kernel, name='grads_last', out_shape=(shape((10...  9.2 us
    all_to_all x1, starting transfers between devices, device_pass(): got = lax.all_to_all(dx_part, ('tp', 'dp'), 0, 0, tiled=True)  3.17 us
  transfers between devices with their start and end apart: 1, of which 0 were waited for; matrix products, arithmetic and copies ran while one was open for 0% of the time, Pallas kernels for 14%

profile of v5, /device:TPU:0, one launch (start us, length us, event | category | flops | bytes accessed | tf_op | source)
XLA Modules:
  0.0 115.2 jit_solution(10226804495849326069)
XLA Ops:
  0.6 85.8 %front.1 = (bf16[2,128,5504]{2,1,0:T(8,128)(2,1)}, bf16[5504,128]{1,0:T(8,128)(2,1)}, bf16[1024,128]{1,0:T(8,128)(2,1)}, bf16[128,1024]{1,0:T(8,128)(2,1)}, bf16...) custom-call(bf16[32,4096]{1,0:T(8,128)(2,1)} %x_hbm.1, bf16[32,4096]{1,0:T(8,128)(2,1)} %dy_hbm.3, ...), custom_call_target="tpu_custom_call" | custom-call | flops 8999999488 | bytes 40000000 | tf_op jit(solution)/shard_map/front/pallas_call | solution.py:535
  86.4 3.2 %all-to-all-start = ((f32[8,32,1024]{2,1,0:T(8,128)}), f32[8,32,1024]{2,1,0:T(8,128)}, u32[]{:S(2)}, u32[]{:S(2)}) async-start(f32[8,32,1024]{2,1,0:T(8,128)} %get-tuple-element.19), calls=%async_computation | async-start | bytes 2097152 | tf_op jit(solution)/shard_map/all_to_all | solution.py:698
  89.6 16.2 %grads_first.1 = (f32[5504,1024]{1,0:T(8,128)}, f32[1024,5504]{1,0:T(8,128)}) custom-call(bf16[5504,128]{1,0:T(8,128)(2,1)} %get-tuple-element.22.act_t_hbm, bf16[128,1024]{1,0:T(8,128)(2,1)} %get-tuple-element.23.dy_cols_hbm, bf16[1024,128]{1,0:T(8,128)(2,1)} %get-tuple-element.16.cols_t_hbm, bf16[2,128,5504]{2,1,0:T(8,128)(2,1)} %get-tuple-element.17.act_hbm), custom_call_target="tpu_custom_call" | custom-call | flops 20000000000 | bytes 50000000 | tf_op jit(solution)/shard_map/grads_first/pallas_call | solution.py:645
  105.8 0.0 all-to-all-done.got_hbm
  105.8 9.2 %grads_last.1 = (f32[1024,5504]{1,0:T(8,128)}, bf16[32,4096]{1,0:T(8,128)(2,1)}, bf16[32,4096]{1,0:T(8,128)(2,1)}) custom-call(bf16[1024,128]{1,0:T(8,128)(2,1)} %get-tuple-element.16.cols_t_hbm, bf16[2,128,5504]{2,1,0:T(8,128)(2,1)} %get-tuple-element.17.act_hbm, bf16[32,4096]{1,0:T(8,128)(2,1)} %get-tuple-element.18.y_hbm, bf16[32,4096]{1,0:T(8,128)(2,1)} %dy_hbm.3, ...), custom_call_target="tpu_custom_call" | custom-call | flops 10000000000 | bytes 30000000 | tf_op jit(solution)/shard_map/grads_last/pallas_call | solution.py:681
Async XLA Ops:
  86.4 19.4 %all-to-all-start = ((f32[8,32,1024]{2,1,0:T(8,128)}), f32[8,32,1024]{2,1,0:T(8,128)}, u32[]{:S(2)}, u32[]{:S(2)}) async-start(f32[8,32,1024]{2,1,0:T(8,128)} %get-tuple-element.19), calls=%async_computation | async-start | bytes 2097152 | tf_op jit(solution)/shard_map/all_to_all | solution.py:698

commit v6 on v5

--- a/solution.py
+++ b/solution.py
@@ -213,7 +213,7 @@
 
 
 def front_kernel(x_hbm, dy_hbm, wg_hbm, wu_hbm, wd_hbm,
-                 act_out, act_t_out, cols_t_out, dy_cols_out, y_out, dx_out,
+                 da_out, db_out, act_t_out, cols_t_out, dy_cols_out, y_out, dx_out,
                  x_ref, dy_ref, wg, wu, wd, part, from_sib, from_opp, act, act_t, cols, cols_t, y_acc, dx_acc, y_got, y_ready,
                  in_sem, gu_sem, d_sem, x_send, x_recv, a0_s, a0_r, a1_s, a1_r, a2_s, a2_r, g1_s, g1_r, g2_s, g2_r,
                  h_sems, q_sems, sum_s, sum_r, row_s, row_r, t_sem, q_sem, o_sem, dx_sem):
@@ -429,15 +429,17 @@
         column_tiles(GG[k], body)
         qg.send(k)
 
-    def act_store(k):
+    def act_stores(k):
         cs = cols_of(GG[k])
-        return pltpu.make_async_copy(act.at[pl.ds(1, 2), :, cs], act_out.at[:, :, cs], q_sem.at[k])
+        return (pltpu.make_async_copy(act.at[1, :, cs], da_out.at[:, cs], q_sem.at[0, k]),
+                pltpu.make_async_copy(act.at[2, :, cs], db_out.at[:, cs], q_sem.at[1, k]))
 
     def dx_part(k, n):
         cs, ns = cols_of(GG[k]), pl.ds(n * MW, MW)
         if n == 0:
             qg.arrived(k)
-            act_store(k).start()
+            for store in act_stores(k):
+                store.start()
         dx = dot_nt(act[1, :, cs], wg[ns, cs]) + dot_nt(act[2, :, cs], wu[ns, cs])
         dx_acc[:, ns] = dx if k == 0 else dx_acc[:, ns] + dx
 
@@ -511,7 +513,8 @@
     for k in range(NG):
         g1(k).wait_send()
         g2(k).wait_send()
-        act_store(k).wait()
+        for store in act_stores(k):
+            store.wait()
     hg.drain()
     qg.drain()
     ysum.drain()
@@ -525,6 +528,7 @@
 DMA = pltpu.SemaphoreType.DMA
 ANY = pl.BlockSpec(memory_space=pl.ANY)
 VMEM = pl.BlockSpec(memory_space=pltpu.VMEM)
+HBM = pl.BlockSpec(memory_space=pltpu.HBM)
 
 
 def shape(dims, dtype):
@@ -535,10 +539,10 @@
     return pl.pallas_call(
         front_kernel,
         name='front',
-        out_shape=(shape((2, 128, HID), BF16), shape((HID, 128), BF16), shape((1024, 128), BF16),
+        out_shape=(shape((128, HID), BF16), shape((128, HID), BF16), shape((HID, 128), BF16), shape((1024, 128), BF16),
                    shape((128, 1024), BF16), shape((32, 4096), BF16), shape((8, 32, 1024), F32)),
         in_specs=[ANY] * 5,
-        out_specs=(ANY,) * 6,
+        out_specs=(ANY,) * 7,
         scratch_shapes=[
             pltpu.VMEM((32, 4096), BF16), pltpu.VMEM((32, 4096), BF16),
             pltpu.VMEM((1024, HID), BF16), pltpu.VMEM((1024, HID), BF16), pltpu.VMEM((HID, 1024), BF16),
@@ -550,7 +554,7 @@
             DMA((2,)), DMA((2,)), DMA((NA,)), DMA((NA,)), DMA((NA,)), DMA((NA,)),
             DMA((NG,)), DMA((NG,)), DMA((NG,)), DMA((NG,)),
             DMA((6, NA)), DMA((6, NG)), DMA((NT,)), DMA((NT,)), DMA((NT, 4)), DMA((NT, 4)),
-            DMA((NA,)), DMA((NG,)), DMA((2,)), DMA((2, 8)),
+            DMA((NA,)), DMA((2, NG)), DMA((2,)), DMA((2, 8)),
         ],
         compiler_params=pltpu.CompilerParams(collective_id=0, has_side_effects=True, vmem_limit_bytes=VMEM_CAP),
         cost_estimate=pl.CostEstimate(flops=9 * 10**9, bytes_accessed=4 * 10**7, transcendentals=0),
@@ -559,13 +563,15 @@
 
 TILE = 512
 SLOTS = 6
-
-
-def stream_tiles(compute, store, width, rest):
+MIB = 1 << 20
+
+
+def stream_tiles(compute, store, width, rest=None):
     full, last = width // TILE, width % TILE
     compute(0, 0, TILE)
     store(0, 0, TILE).start()
-    rest()
+    if rest is not None:
+        rest()
 
     def step(i, carry):
         slot = lax.rem(i, SLOTS)
@@ -594,26 +600,14 @@
     return drain
 
 
-def load_all(pairs, sem):
-    loads = [pltpu.make_async_copy(src, dst, sem.at[n]) for n, (src, dst) in enumerate(pairs)]
-    for load in loads:
-        load.start()
-
-    def wait(*which):
-        for n in which:
-            loads[n].wait()
-
-    return wait
-
-
-def column_job(left, right, ring, out, base, sem):
+def column_job(left, right, ring, out, sem):
     def compute(i, slot, width):
         cs = pl.ds(aligned(i * TILE, 128), width)
         ring[slot, :, pl.ds(0, width)] = dot_nn(left[...], right[:, cs])
 
     def store(i, slot, width):
         return pltpu.make_async_copy(ring.at[slot, :, pl.ds(0, width)],
-                                     out.at[:, pl.ds(aligned(base + i * TILE, 128), width)], sem.at[slot])
+                                     out.at[:, pl.ds(aligned(i * TILE, 128), width)], sem.at[slot])
 
     return compute, store
 
@@ -629,43 +623,45 @@
     return compute, store
 
 
-def grads_first_kernel(act_t_hbm, dy_cols_hbm, cols_t_hbm, act_hbm, down_out, gate_out,
-                       act_t, dy_cols, cols_t, act, ring_d, ring_c, in_sem, sem_d, sem_c):
+def grads_first_kernel(act_t_hbm, dy_cols_hbm, cols_t_hbm, da_hbm, down_out, gate_out,
+                       act_t, dy_cols, cols_t, da, ring_d, ring_c, in_sem, sem_d, sem_c):
     head, tail = pl.ds(0, TILE), pl.ds(TILE, HID - TILE)
-    wait = load_all(((dy_cols_hbm, dy_cols), (act_t_hbm.at[head, :], act_t.at[head, :]),
-                     (act_t_hbm.at[tail, :], act_t.at[tail, :]), (cols_t_hbm, cols_t), (act_hbm.at[0], act)), in_sem)
-    wait(0, 1)
-    drain_d = stream_tiles(*row_job(act_t, dy_cols, ring_d, down_out, sem_d), HID, lambda: wait(2, 3, 4))
-    drain_c = stream_tiles(*column_job(cols_t, act, ring_c, gate_out, 0, sem_c), HID, lambda: None)
+    pairs = ((dy_cols_hbm, dy_cols), (act_t_hbm.at[head, :], act_t.at[head, :]),
+             (act_t_hbm.at[tail, :], act_t.at[tail, :]), (cols_t_hbm, cols_t), (da_hbm, da))
+    loads = [pltpu.make_async_copy(src, dst, in_sem.at[n]) for n, (src, dst) in enumerate(pairs)]
+    for load in loads:
+        load.start()
+
+    def rest():
+        for load in loads[2:]:
+            load.wait()
+
+    loads[0].wait()
+    loads[1].wait()
+    drain_d = stream_tiles(*row_job(act_t, dy_cols, ring_d, down_out, sem_d), HID, rest)
+    drain_c = stream_tiles(*column_job(cols_t, da, ring_c, gate_out, sem_c), HID)
     drain_d()
     drain_c()
 
 
-def grads_first(act_t, dy_cols, cols_t, act):
+def grads_first(act_t, dy_cols, cols_t, da):
     return pl.pallas_call(
         grads_first_kernel,
         name='grads_first',
         out_shape=(shape((HID, 1024), F32), shape((1024, HID), F32)),
-        in_specs=[ANY] * 4,
+        in_specs=[HBM] * 4,
         out_specs=(ANY,) * 2,
         scratch_shapes=[pltpu.VMEM((HID, 128), BF16), pltpu.VMEM((128, 1024), BF16), pltpu.VMEM((1024, 128), BF16),
                         pltpu.VMEM((128, HID), BF16),
                         pltpu.VMEM((SLOTS, TILE, 1024), F32), pltpu.VMEM((SLOTS, 1024, TILE), F32),
                         DMA((5,)), DMA((SLOTS,)), DMA((SLOTS,))],
-        compiler_params=pltpu.CompilerParams(vmem_limit_bytes=VMEM_CAP),
+        compiler_params=pltpu.CompilerParams(vmem_limit_bytes=60 * MIB),
         cost_estimate=pl.CostEstimate(flops=2 * 10**10, bytes_accessed=5 * 10**7, transcendentals=0),
-    )(act_t, dy_cols, cols_t, act)
-
-
-def grads_last_kernel(cols_t_hbm, act_hbm, y_hbm, dy_hbm, got_hbm, up_out, y_out, dx_out,
-                      cols_t, act, y_rows, dy_rows, got, dx_rows, ring, in_sem, sem, row_sem):
-    head, tail = pl.ds(0, TILE), pl.ds(TILE, HID - TILE)
-    wait = load_all(((cols_t_hbm, cols_t), (act_hbm.at[1, :, head], act.at[:, head]),
-                     (act_hbm.at[1, :, tail], act.at[:, tail]), (y_hbm, y_rows), (dy_hbm, dy_rows),
-                     (got_hbm, got)), in_sem)
-    wait(0, 1)
-    drain = stream_tiles(*column_job(cols_t, act, ring, up_out, 0, sem), HID, lambda: wait(2))
-    wait(3, 4, 5)
+    )(act_t, dy_cols, cols_t, da)
+
+
+def grads_last_kernel(cols_t, db, y_rows, dy_rows, got, up_out, y_out, dx_out, dx_rows, ring, sem, row_sem):
+    drain = stream_tiles(*column_job(cols_t, db, ring, up_out, sem), HID)
     copies = (pltpu.make_async_copy(y_rows, y_out, row_sem.at[0]), pltpu.make_async_copy(dx_rows, dx_out, row_sem.at[1]))
     copies[0].start()
     for d in range(4):
@@ -677,27 +673,26 @@
         copy.wait()
 
 
-def grads_last(cols_t, act, y, dy, got):
+def grads_last(cols_t, db, y, dy, got):
     return pl.pallas_call(
         grads_last_kernel,
         name='grads_last',
         out_shape=(shape((1024, HID), F32), shape((32, 4096), BF16), shape((32, 4096), BF16)),
-        in_specs=[ANY] * 5,
+        in_specs=[VMEM] * 5,
         out_specs=(ANY,) * 3,
-        scratch_shapes=[pltpu.VMEM((1024, 128), BF16), pltpu.VMEM((128, HID), BF16), pltpu.VMEM((32, 4096), BF16),
-                        pltpu.VMEM((32, 4096), BF16), pltpu.VMEM((8, 32, 1024), F32), pltpu.VMEM((32, 4096), BF16),
-                        pltpu.VMEM((SLOTS, 1024, TILE), F32), DMA((6,)), DMA((SLOTS,)), DMA((2,))],
-        compiler_params=pltpu.CompilerParams(vmem_limit_bytes=VMEM_CAP),
+        scratch_shapes=[pltpu.VMEM((32, 4096), BF16), pltpu.VMEM((SLOTS, 1024, TILE), F32),
+                        DMA((SLOTS,)), DMA((2,))],
+        compiler_params=pltpu.CompilerParams(vmem_limit_bytes=20 * MIB),
         cost_estimate=pl.CostEstimate(flops=10**10, bytes_accessed=3 * 10**7, transcendentals=0),
-    )(cols_t, act, y, dy, got)
+    )(cols_t, db, y, dy, got)
 
 
 def solution(mesh):
     def device_pass(x_rows, gate_blk, up_blk, down_blk, dy_rows):
-        act, act_t, cols_t, dy_cols, y_part, dx_part = front(x_rows, dy_rows, gate_blk, up_blk, down_blk)
+        da, db, act_t, cols_t, dy_cols, y_part, dx_part = front(x_rows, dy_rows, gate_blk, up_blk, down_blk)
         got = lax.all_to_all(dx_part, ('tp', 'dp'), 0, 0, tiled=True)
-        dw_down, dw_gate = grads_first(act_t, dy_cols, cols_t, act)
-        dw_up, y_rows, dx_rows = grads_last(cols_t, act, y_part, dy_rows, got)
+        dw_down, dw_gate = grads_first(act_t, dy_cols, cols_t, da)
+        dw_up, y_rows, dx_rows = grads_last(cols_t, db, y_part, dy_rows, got)
         return y_rows, dx_rows, dw_gate, dw_up, dw_down
 
     row_spec = P('dp', None)

time: 115 us -> 114 us (level)
  no operation moved by 1% of the time
where the time goes in v6:
time: 114 us
  Pallas kernels  110 us (96%)
  starting transfers between devices  2.49 us (2%)
    pallas_call x1, Pallas kernels, front(): pl.pallas_call(front_kernel, name='front', out_shape=(shape((128, HID), B...  85.9 us
    pallas_call x1, Pallas kernels, grads_first(): pl.pallas_call(grads_first_kernel, name='grads_first', out_shape=(shape((...  16.3 us
    pallas_call x1, Pallas kernels, grads_last(): pl.pallas_call(grads_last_kernel, name='grads_last', out_shape=(shape((10...  8.22 us
    all_to_all x1, starting transfers between devices, device_pass(): got = lax.all_to_all(dx_part, ('tp', 'dp'), 0, 0, tiled=True)  2.49 us
  transfers between devices with their start and end apart: 1, of which 0 were waited for; matrix products, arithmetic and copies ran while one was open for 0% of the time, Pallas kernels for 14%

profile of v6, /device:TPU:0, one launch (start us, length us, event | category | flops | bytes accessed | tf_op | source)
XLA Modules:
  0.0 113.8 jit_solution(4603461277865851410)
XLA Ops:
  0.6 85.9 %front.1 = (bf16[128,5504]{1,0:T(8,128)(2,1)}, bf16[128,5504]{1,0:T(8,128)(2,1)}, bf16[5504,128]{1,0:T(8,128)(2,1)}, bf16[1024,128]{1,0:T(8,128)(2,1)}, bf16[128...) custom-call(bf16[32,4096]{1,0:T(8,128)(2,1)} %x_hbm.1, bf16[32,4096]{1,0:T(8,128)(2,1)} %dy_rows.1, ...), custom_call_target="tpu_custom_call" | custom-call | flops 8999999488 | bytes 40000000 | tf_op jit(solution)/shard_map/front/pallas_call | solution.py:539
  86.5 2.5 %all-to-all-start = ((f32[8,32,1024]{2,1,0:T(8,128)}), f32[8,32,1024]{2,1,0:T(8,128)S(1)}, u32[]{:S(2)}, u32[]{:S(2)}) async-start(f32[8,32,1024]{2,1,0:T(8,128)} %get-tuple-element.20), calls=%async_computation | async-start | bytes 2097152 | tf_op jit(solution)/shard_map/all_to_all | solution.py:693
  89.0 0.0 copy-start
  89.0 0.0 copy-start.1
  89.0 0.0 copy-start.2
  89.0 0.0 copy-start.3
  89.0 16.3 %grads_first.1 = (f32[5504,1024]{1,0:T(8,128)}, f32[1024,5504]{1,0:T(8,128)}) custom-call(bf16[5504,128]{1,0:T(8,128)(2,1)} %get-tuple-element.23.act_t_hbm, bf16[128,1024]{1,0:T(8,128)(2,1)} %get-tuple-element.24.dy_cols_hbm, bf16[1024,128]{1,0:T(8,128)(2,1)} %get-tuple-element.17.cols_t.cols_t_hbm, bf16[128,5504]{1,0:T(8,128)(2,1)} %get-tuple-element.25.da_hbm), custom_call_target="tpu_custom_call" | custom-call | flops 20000000000 | bytes 50000000 | tf_op jit(solution)/shard_map/grads_first/pallas_call | solution.py:648
  105.4 0.0 all-to-all-done.got
  105.4 0.0 copy-done
  105.4 0.0 copy-done.1
  105.4 0.0 copy-done.2
  105.4 0.0 copy-done.3
  105.4 8.2 %grads_last.1 = (f32[1024,5504]{1,0:T(8,128)}, bf16[32,4096]{1,0:T(8,128)(2,1)}, bf16[32,4096]{1,0:T(8,128)(2,1)}) custom-call(bf16[1024,128]{1,0:T(8,128)(2,1)S(1)} %copy-done.2, bf16[128,5504]{1,0:T(8,128)(2,1)S(1)} %copy-done.1, bf16[32,4096]{1,0:T(8,128)(2,1)S(1)} %copy-done.3, bf16[32,4096]{1,0:T(8,128)(2,1)S(1)} %copy-done, ...), custom_call_target="tpu_custom_call" | custom-call | flops 10000000000 | bytes 30000000 | tf_op jit(solution)/shard_map/grads_last/pallas_call | solution.py:677
Async XLA Ops:
  86.5 18.9 %all-to-all-start = ((f32[8,32,1024]{2,1,0:T(8,128)}), f32[8,32,1024]{2,1,0:T(8,128)S(1)}, u32[]{:S(2)}, u32[]{:S(2)}) async-start(f32[8,32,1024]{2,1,0:T(8,128)} %get-tuple-element.20), calls=%async_computation | async-start | bytes 2097152 | tf_op jit(solution)/shard_map/all_to_all | solution.py:693
  89.0 16.4 %copy-start = (bf16[32,4096]{1,0:T(8,128)(2,1)S(1)}, bf16[32,4096]{1,0:T(8,128)(2,1)}, u32[]{:S(2)}) copy-start(bf16[32,4096]{1,0:T(8,128)(2,1)} %dy_rows.1) | copy-start | bytes 786436
  89.0 16.4 %copy-start.1 = (bf16[128,5504]{1,0:T(8,128)(2,1)S(1)}, bf16[128,5504]{1,0:T(8,128)(2,1)}, u32[]{:S(2)}) copy-start(bf16[128,5504]{1,0:T(8,128)(2,1)} %get-tuple-element.18.db) | copy-start | bytes 4227076
  89.0 16.4 %copy-start.2 = (bf16[1024,128]{1,0:T(8,128)(2,1)S(1)}, bf16[1024,128]{1,0:T(8,128)(2,1)}, u32[]{:S(2)}) copy-start(bf16[1024,128]{1,0:T(8,128)(2,1)} %get-tuple-element.17.cols_t.cols_t_hbm) | copy-start | bytes 786436
  89.0 16.4 %copy-start.3 = (bf16[32,4096]{1,0:T(8,128)(2,1)S(1)}, bf16[32,4096]{1,0:T(8,128)(2,1)}, u32[]{:S(2)}) copy-start(bf16[32,4096]{1,0:T(8,128)(2,1)} %get-tuple-element.19.y_rows) | copy-start | bytes 786436

commit v7 on v6

--- a/solution.py
+++ b/solution.py
@@ -20,7 +20,7 @@
 
 
 AB = chunks(0, (512, 512, 1024, 1024, 1024, 1024, 384))
-GG = chunks(0, (512, 1024, 1024, 1024, 1024, 512, 256, 128))
+GG = chunks(0, (512, 1024, 1024, 1024, 768, 640, 384, 128))
 NA, NG = len(AB), len(GG)
 NT = 4
 TW = 1024 // NT
@@ -486,8 +486,8 @@
         ysum.finish(n)
     for n in range(NT):
         ysum.row_copy(n, 1, 0).start()
-    for step in ('f0', 'f1', 'd0', 'D0', 'f2', 'd1', 'D1', 'd2', 'f3', 'D2', 'f4', 'd3', 'f5', 'D3', 'f6', 'f7',
-                 'd4', 'D4', 'd5', 'D5', 'd6', 'D6', 'd7'):
+    for step in ('f0', 'f1', 'd0', 'D0', 'f2', 'd1', 'D1', 'f3', 'd2', 'D2', 'f4', 'd3', 'D3', 'f5', 'd4', 'f6', 'D4',
+                 'f7', 'd5', 'D5', 'd6', 'D6', 'd7'):
         k = int(step[1])
         if step[0] == 'f':
             qg.forward(k)

time: 114 us -> 113 us (level)
  no operation moved by 1% of the time
where the time goes in v7:
time: 113 us
  Pallas kernels  110 us (97%)
  starting transfers between devices  2.49 us (2%)
    pallas_call x1, Pallas kernels, front(): pl.pallas_call(front_kernel, name='front', out_shape=(shape((128, HID), B...  85 us
    pallas_call x1, Pallas kernels, grads_first(): pl.pallas_call(grads_first_kernel, name='grads_first', out_shape=(shape((...  16.3 us
    pallas_call x1, Pallas kernels, grads_last(): pl.pallas_call(grads_last_kernel, name='grads_last', out_shape=(shape((10...  8.22 us
    all_to_all x1, starting transfers between devices, device_pass(): got = lax.all_to_all(dx_part, ('tp', 'dp'), 0, 0, tiled=True)  2.49 us
  transfers between devices with their start and end apart: 1, of which 0 were waited for; matrix products, arithmetic and copies ran while one was open for 0% of the time, Pallas kernels for 14%

profile of v7, /device:TPU:0, one launch (start us, length us, event | category | flops | bytes accessed | tf_op | source)
XLA Modules:
  0.0 112.9 jit_solution(12059635986149303502)
XLA Ops:
  0.6 85.0 %front.1 = (bf16[128,5504]{1,0:T(8,128)(2,1)}, bf16[128,5504]{1,0:T(8,128)(2,1)}, bf16[5504,128]{1,0:T(8,128)(2,1)}, bf16[1024,128]{1,0:T(8,128)(2,1)}, bf16[128...) custom-call(bf16[32,4096]{1,0:T(8,128)(2,1)} %x_hbm.1, bf16[32,4096]{1,0:T(8,128)(2,1)} %dy_rows.1, ...), custom_call_target="tpu_custom_call" | custom-call | flops 8999999488 | bytes 40000000 | tf_op jit(solution)/shard_map/front/pallas_call | solution.py:539
  85.6 2.5 %all-to-all-start = ((f32[8,32,1024]{2,1,0:T(8,128)}), f32[8,32,1024]{2,1,0:T(8,128)S(1)}, u32[]{:S(2)}, u32[]{:S(2)}) async-start(f32[8,32,1024]{2,1,0:T(8,128)} %get-tuple-element.20), calls=%async_computation | async-start | bytes 2097152 | tf_op jit(solution)/shard_map/all_to_all | solution.py:693
  88.1 0.0 copy-start
  88.1 0.0 copy-start.1
  88.1 0.0 copy-start.2
  88.2 0.0 copy-start.3
  88.2 16.3 %grads_first.1 = (f32[5504,1024]{1,0:T(8,128)}, f32[1024,5504]{1,0:T(8,128)}) custom-call(bf16[5504,128]{1,0:T(8,128)(2,1)} %get-tuple-element.23.act_t_hbm, bf16[128,1024]{1,0:T(8,128)(2,1)} %get-tuple-element.24.dy_cols_hbm, bf16[1024,128]{1,0:T(8,128)(2,1)} %get-tuple-element.17.cols_t.cols_t_hbm, bf16[128,5504]{1,0:T(8,128)(2,1)} %get-tuple-element.25.da_hbm), custom_call_target="tpu_custom_call" | custom-call | flops 20000000000 | bytes 50000000 | tf_op jit(solution)/shard_map/grads_first/pallas_call | solution.py:648
  104.5 0.0 all-to-all-done.got
  104.5 0.0 copy-done
  104.5 0.0 copy-done.1
  104.5 0.0 copy-done.2
  104.5 0.0 copy-done.3
  104.5 8.2 %grads_last.1 = (f32[1024,5504]{1,0:T(8,128)}, bf16[32,4096]{1,0:T(8,128)(2,1)}, bf16[32,4096]{1,0:T(8,128)(2,1)}) custom-call(bf16[1024,128]{1,0:T(8,128)(2,1)S(1)} %copy-done.2, bf16[128,5504]{1,0:T(8,128)(2,1)S(1)} %copy-done.1, bf16[32,4096]{1,0:T(8,128)(2,1)S(1)} %copy-done.3, bf16[32,4096]{1,0:T(8,128)(2,1)S(1)} %copy-done, ...), custom_call_target="tpu_custom_call" | custom-call | flops 10000000000 | bytes 30000000 | tf_op jit(solution)/shard_map/grads_last/pallas_call | solution.py:677
Async XLA Ops:
  85.6 18.9 %all-to-all-start = ((f32[8,32,1024]{2,1,0:T(8,128)}), f32[8,32,1024]{2,1,0:T(8,128)S(1)}, u32[]{:S(2)}, u32[]{:S(2)}) async-start(f32[8,32,1024]{2,1,0:T(8,128)} %get-tuple-element.20), calls=%async_computation | async-start | bytes 2097152 | tf_op jit(solution)/shard_map/all_to_all | solution.py:693
  88.1 16.4 %copy-start = (bf16[32,4096]{1,0:T(8,128)(2,1)S(1)}, bf16[32,4096]{1,0:T(8,128)(2,1)}, u32[]{:S(2)}) copy-start(bf16[32,4096]{1,0:T(8,128)(2,1)} %dy_rows.1) | copy-start | bytes 786436
  88.1 16.4 %copy-start.1 = (bf16[128,5504]{1,0:T(8,128)(2,1)S(1)}, bf16[128,5504]{1,0:T(8,128)(2,1)}, u32[]{:S(2)}) copy-start(bf16[128,5504]{1,0:T(8,128)(2,1)} %get-tuple-element.18.db) | copy-start | bytes 4227076
  88.1 16.4 %copy-start.2 = (bf16[1024,128]{1,0:T(8,128)(2,1)S(1)}, bf16[1024,128]{1,0:T(8,128)(2,1)}, u32[]{:S(2)}) copy-start(bf16[1024,128]{1,0:T(8,128)(2,1)} %get-tuple-element.17.cols_t.cols_t_hbm) | copy-start | bytes 786436
  88.2 16.4 %copy-start.3 = (bf16[32,4096]{1,0:T(8,128)(2,1)S(1)}, bf16[32,4096]{1,0:T(8,128)(2,1)}, u32[]{:S(2)}) copy-start(bf16[32,4096]{1,0:T(8,128)(2,1)} %get-tuple-element.19.y_rows) | copy-start | bytes 786436

commit v8 on v7

--- a/solution.py
+++ b/solution.py
@@ -568,8 +568,9 @@
 
 def stream_tiles(compute, store, width, rest=None):
     full, last = width // TILE, width % TILE
-    compute(0, 0, TILE)
-    store(0, 0, TILE).start()
+    for off in range(0, TILE, 128):
+        compute(0, 0, 128, off)
+        store(0, 0, 128, off).start()
     if rest is not None:
         rest()
 
@@ -601,24 +602,24 @@
 
 
 def column_job(left, right, ring, out, sem):
-    def compute(i, slot, width):
-        cs = pl.ds(aligned(i * TILE, 128), width)
-        ring[slot, :, pl.ds(0, width)] = dot_nn(left[...], right[:, cs])
-
-    def store(i, slot, width):
-        return pltpu.make_async_copy(ring.at[slot, :, pl.ds(0, width)],
-                                     out.at[:, pl.ds(aligned(i * TILE, 128), width)], sem.at[slot])
+    def compute(i, slot, width, off=0):
+        cs = pl.ds(aligned(i * TILE + off, 128), width)
+        ring[slot, :, pl.ds(off, width)] = dot_nn(left[...], right[:, cs])
+
+    def store(i, slot, width, off=0):
+        return pltpu.make_async_copy(ring.at[slot, :, pl.ds(off, width)],
+                                     out.at[:, pl.ds(aligned(i * TILE + off, 128), width)], sem.at[slot])
 
     return compute, store
 
 
 def row_job(left, right, ring, out, sem):
-    def compute(i, slot, width):
-        ring[slot, pl.ds(0, width), :] = dot_nn(left[pl.ds(aligned(i * TILE, 128), width), :], right[...])
-
-    def store(i, slot, width):
-        return pltpu.make_async_copy(ring.at[slot, pl.ds(0, width), :],
-                                     out.at[pl.ds(aligned(i * TILE, 128), width), :], sem.at[slot])
+    def compute(i, slot, width, off=0):
+        ring[slot, pl.ds(off, width), :] = dot_nn(left[pl.ds(aligned(i * TILE + off, 128), width), :], right[...])
+
+    def store(i, slot, width, off=0):
+        return pltpu.make_async_copy(ring.at[slot, pl.ds(off, width), :],
+                                     out.at[pl.ds(aligned(i * TILE + off, 128), width), :], sem.at[slot])
 
     return compute, store
 

time: 113 us -> 113 us (level)
  no operation moved by 1% of the time
where the time goes in v8:
time: 113 us
  Pallas kernels  109 us (96%)
  starting transfers between devices  2.49 us (2%)
    pallas_call x1, Pallas kernels, front(): pl.pallas_call(front_kernel, name='front', out_shape=(shape((128, HID), B...  85 us
    pallas_call x1, Pallas kernels, grads_first(): pl.pallas_call(grads_first_kernel, name='grads_first', out_shape=(shape((...  16.3 us
    pallas_call x1, Pallas kernels, grads_last(): pl.pallas_call(grads_last_kernel, name='grads_last', out_shape=(shape((10...  8.1 us
    all_to_all x1, starting transfers between devices, device_pass(): got = lax.all_to_all(dx_part, ('tp', 'dp'), 0, 0, tiled=True)  2.49 us
  transfers between devices with their start and end apart: 1, of which 0 were waited for; matrix products, arithmetic and copies ran while one was open for 0% of the time, Pallas kernels for 14%

profile of v8, /device:TPU:0, one launch (start us, length us, event | category | flops | bytes accessed | tf_op | source)
XLA Modules:
  0.0 112.8 jit_solution(5850134342206959262)
XLA Ops:
  0.6 85.0 %front.1 = (bf16[128,5504]{1,0:T(8,128)(2,1)}, bf16[128,5504]{1,0:T(8,128)(2,1)}, bf16[5504,128]{1,0:T(8,128)(2,1)}, bf16[1024,128]{1,0:T(8,128)(2,1)}, bf16[128...) custom-call(bf16[32,4096]{1,0:T(8,128)(2,1)} %x_hbm.1, bf16[32,4096]{1,0:T(8,128)(2,1)} %dy_rows.1, ...), custom_call_target="tpu_custom_call" | custom-call | flops 8999999488 | bytes 40000000 | tf_op jit(solution)/shard_map/front/pallas_call | solution.py:539
  85.6 2.5 %all-to-all-start = ((f32[8,32,1024]{2,1,0:T(8,128)}), f32[8,32,1024]{2,1,0:T(8,128)S(1)}, u32[]{:S(2)}, u32[]{:S(2)}) async-start(f32[8,32,1024]{2,1,0:T(8,128)} %get-tuple-element.20), calls=%async_computation | async-start | bytes 2097152 | tf_op jit(solution)/shard_map/all_to_all | solution.py:694
  88.1 0.0 copy-start
  88.1 0.0 copy-start.1
  88.1 0.0 copy-start.2
  88.2 0.0 copy-start.3
  88.2 16.3 %grads_first.1 = (f32[5504,1024]{1,0:T(8,128)}, f32[1024,5504]{1,0:T(8,128)}) custom-call(bf16[5504,128]{1,0:T(8,128)(2,1)} %get-tuple-element.23.act_t_hbm, bf16[128,1024]{1,0:T(8,128)(2,1)} %get-tuple-element.24.dy_cols_hbm, bf16[1024,128]{1,0:T(8,128)(2,1)} %get-tuple-element.17.cols_t.cols_t_hbm, bf16[128,5504]{1,0:T(8,128)(2,1)} %get-tuple-element.25.da_hbm), custom_call_target="tpu_custom_call" | custom-call | flops 20000000000 | bytes 50000000 | tf_op jit(solution)/shard_map/grads_first/pallas_call | solution.py:649
  104.5 0.0 all-to-all-done.got
  104.5 0.0 copy-done
  104.5 0.0 copy-done.1
  104.5 0.0 copy-done.2
  104.5 0.0 copy-done.3
  104.5 8.1 %grads_last.1 = (f32[1024,5504]{1,0:T(8,128)}, bf16[32,4096]{1,0:T(8,128)(2,1)}, bf16[32,4096]{1,0:T(8,128)(2,1)}) custom-call(bf16[1024,128]{1,0:T(8,128)(2,1)S(1)} %copy-done.2, bf16[128,5504]{1,0:T(8,128)(2,1)S(1)} %copy-done.1, bf16[32,4096]{1,0:T(8,128)(2,1)S(1)} %copy-done.3, bf16[32,4096]{1,0:T(8,128)(2,1)S(1)} %copy-done, ...), custom_call_target="tpu_custom_call" | custom-call | flops 10000000000 | bytes 30000000 | tf_op jit(solution)/shard_map/grads_last/pallas_call | solution.py:678
Async XLA Ops:
  85.6 18.9 %all-to-all-start = ((f32[8,32,1024]{2,1,0:T(8,128)}), f32[8,32,1024]{2,1,0:T(8,128)S(1)}, u32[]{:S(2)}, u32[]{:S(2)}) async-start(f32[8,32,1024]{2,1,0:T(8,128)} %get-tuple-element.20), calls=%async_computation | async-start | bytes 2097152 | tf_op jit(solution)/shard_map/all_to_all | solution.py:694
  88.1 16.4 %copy-start = (bf16[32,4096]{1,0:T(8,128)(2,1)S(1)}, bf16[32,4096]{1,0:T(8,128)(2,1)}, u32[]{:S(2)}) copy-start(bf16[32,4096]{1,0:T(8,128)(2,1)} %dy_rows.1) | copy-start | bytes 786436
  88.1 16.4 %copy-start.1 = (bf16[128,5504]{1,0:T(8,128)(2,1)S(1)}, bf16[128,5504]{1,0:T(8,128)(2,1)}, u32[]{:S(2)}) copy-start(bf16[128,5504]{1,0:T(8,128)(2,1)} %get-tuple-element.18.db) | copy-start | bytes 4227076
  88.1 16.4 %copy-start.2 = (bf16[1024,128]{1,0:T(8,128)(2,1)S(1)}, bf16[1024,128]{1,0:T(8,128)(2,1)}, u32[]{:S(2)}) copy-start(bf16[1024,128]{1,0:T(8,128)(2,1)} %get-tuple-element.17.cols_t.cols_t_hbm) | copy-start | bytes 786436
  88.2 16.4 %copy-start.3 = (bf16[32,4096]{1,0:T(8,128)(2,1)S(1)}, bf16[32,4096]{1,0:T(8,128)(2,1)}, u32[]{:S(2)}) copy-start(bf16[32,4096]{1,0:T(8,128)(2,1)} %get-tuple-element.19.y_rows) | copy-start | bytes 786436
